TPU v7x, 512 devices: a 4x2x32 block of a 4x8x32 slice. The times are simulated.
512 devices in a mesh: grp: 2 (over y), smp: 32 (over z), blk: 4 (over x), pen: 2 (over core).
Axes of the slice: x: 4, y: 2, z: 32, core: 2. Of those that a mesh axis runs over, the one named last changes fastest.
The devices are a block of a 4x8x32 slice.
Arguments:
- allele_matrix: bfloat16 [16384, 8192], P('smp', ('grp', 'blk')), parts along dimension 1, may hold values from -6 to 6
- orthonormal_frames: bfloat16 [16, 512, 512], P(('grp', 'blk')), parts along dimension 0, may hold values from -0.25 to 0.25
- segment_variances: float32 [16, 512], P(('grp', 'blk')), parts along dimension 0, may hold values from 163.84 to 16384
- lambda_grid: float32 [4], replicated, may hold values from 163.84 to 16384
- trait_levels: bfloat16 [16384, 256], P('smp', ('grp', 'pen')), parts along dimension 1, may hold values from -6 to 6
- partition_labels: int32 [16384], P('smp'), may hold values from 0 to 3
- preceding_fits: bfloat16 [4, 16384, 1536], P(('grp', 'pen'), 'smp', 'blk'), parts along dimension 0, may hold values from -6 to 6
Outputs:
- level0_predictions: bfloat16 [16384, 16, 4, 128], P('smp', ('grp', 'blk'), None, 'pen'), parts along dimension 1
- gram_old: float32 [4, 1536, 1536], P(('grp', 'pen'), 'blk', 'smp'), parts along dimension 0
- gram_cross: float32 [4, 32, 1536], P(('grp', 'pen'), 'blk', 'smp'), parts along dimension 0
- gram_new: float32 [4, 32, 32], P(('grp', 'pen'), 'blk'), parts along dimension 0
- fit_old: float32 [4, 1536], P(('grp', 'pen'), 'smp'), parts along dimension 0
- fit_new: float32 [4, 32], P(('grp', 'pen'), 'blk'), parts along dimension 0
There are 2 independent parts, one for each index of `grp`. A program takes and returns all parts, laid end to end along the dimension named above; an argument that names none is the same for every part. Nothing has to cross between parts.
All inputs are finite; a program needn't handle non-finite values.
Results may differ from a plain program's by a relative error of at most 0.018.
Values may be sent and summed in bfloat16 or wider, within the bound.
No kernel may reach another device: no remote copies, remote signals or barrier semaphores. Data moves between devices by JAX's collectives and lax.ppermute only.
A program may use at most 64 MiB of HBM per device.

v0:
```python
import jax
import jax.numpy as jnp
from jax import lax
from jax.sharding import PartitionSpec as P

FOLDS = 4


def in_order(blocks, dim):
    blocks = jnp.moveaxis(blocks, 0, dim)
    shape = blocks.shape
    return blocks.reshape(*shape[:dim], shape[dim] * shape[dim + 1], *shape[dim + 2 :])


def copy_for_each(shard, axis):
    count = lax.axis_size(axis)
    return lax.all_to_all(
        jnp.broadcast_to(shard[None], (count, *shard.shape)), axis, 0, 0, tiled=True
    )


def gather_directly(shard, axis, dim):
    return in_order(copy_for_each(shard, axis), dim)


def split_up(shard, dim, count):
    before, after = (shard.shape[:dim], shard.shape[dim + 1 :])
    return jnp.moveaxis(shard.reshape(*before, count, -1, *after), dim, 0)


def summed_on_arrival(shard, axis, dim):
    blocks = split_up(shard, dim, lax.axis_size(axis))
    arrived = lax.all_to_all(blocks, axis, split_axis=0, concat_axis=0, tiled=True)
    return arrived.sum(axis=0)


def taken_together(shard, axis):
    everything = copy_for_each(shard, axis)
    return jnp.sum(everything, axis=0)


def segment_fitted_trait(
    projected_traits, pairwise_inner, spectral_line, lambda_grid, partition_mask_real
):
    var_width = projected_traits.shape[1]
    prot_width = pairwise_inner.shape[1] // FOLDS
    lambda_grid_size = lambda_grid.shape[0]
    pairwise_inner = pairwise_inner.reshape(var_width, FOLDS, prot_width)
    remainder = jnp.sum(pairwise_inner, axis=1, keepdims=True) - pairwise_inner
    damping_ratio = 1.0 / (spectral_line[:, None] + lambda_grid[None, :])
    ridge_coefficients = (remainder[:, :, None, :] * damping_ratio[:, None, :, None]).astype(
        jnp.bfloat16
    )
    row_count = projected_traits.shape[0]
    running_total = jnp.zeros((row_count, lambda_grid_size * prot_width), jnp.float32)
    for holdout_index in range(FOLDS):
        lookup_table = ridge_coefficients[:, holdout_index].reshape(
            var_width, lambda_grid_size * prot_width
        )
        running_total = running_total + partition_mask_real[
            :, holdout_index : holdout_index + 1
        ] * jnp.dot(projected_traits, lookup_table, preferred_element_type=jnp.float32)
    return running_total.reshape(row_count, lambda_grid_size, prot_width).astype(jnp.bfloat16)


def per_device(
    allele_matrix,
    orthonormal_frames,
    segment_variances,
    lambda_grid,
    trait_levels,
    partition_labels,
    preceding_fits,
):
    row_count = allele_matrix.shape[0]
    block_count = orthonormal_frames.shape[0]
    var_width = orthonormal_frames.shape[1]
    prot_width = trait_levels.shape[1]
    lambda_grid_size = lambda_grid.shape[0]
    sample_total = float(row_count * lax.axis_size("smp"))
    contract = (((0,), (0,)), ((), ()))
    member = partition_labels[:, None] == jnp.arange(FOLDS, dtype=jnp.int32)[None, :]
    partition_mask_real = member.astype(jnp.float32)
    masked = (member.astype(jnp.bfloat16)[:, :, None] * trait_levels[:, None, :]).reshape(
        row_count, FOLDS * prot_width
    )
    rotated_list = []
    local_list = []
    for entry_offset in range(block_count):
        genotype_cols = allele_matrix[:, entry_offset * var_width : (entry_offset + 1) * var_width]
        projected_traits = jnp.dot(
            genotype_cols, orthonormal_frames[entry_offset], preferred_element_type=jnp.float32
        ).astype(jnp.bfloat16)
        rotated_list.append(projected_traits)
        local_list.append(
            lax.dot_general(projected_traits, masked, contract, preferred_element_type=jnp.float32)
        )
    summed = lax.psum(jnp.stack(local_list), "smp")
    crossed_list = [summed[entry_offset] for entry_offset in range(block_count)]
    pred_list = [
        segment_fitted_trait(
            rotated_list[entry_offset],
            crossed_list[entry_offset],
            segment_variances[entry_offset],
            lambda_grid,
            partition_mask_real,
        )
        for entry_offset in range(block_count)
    ]
    level0_predictions = jnp.stack(pred_list, axis=1)
    added_columns = level0_predictions[:, :, :, 0].reshape(
        row_count, block_count * lambda_grid_size
    )
    target = trait_levels[:, 0:1]
    old_cols = preceding_fits[0]
    old_width = old_cols.shape[1]
    new_width = added_columns.shape[1]
    joined = jnp.concatenate([old_cols, added_columns], axis=1)
    gathered = gather_directly(joined, "blk", 1)
    shard_count = gathered.shape[1] // joined.shape[1]
    pieces = gathered.reshape(row_count, shard_count, joined.shape[1])
    old_all = pieces[:, :, :old_width].reshape(row_count, shard_count * old_width)
    new_all = pieces[:, :, old_width:].reshape(row_count, shard_count * new_width)
    gram_old = lax.psum_scatter(
        lax.dot_general(old_cols, old_all, contract, preferred_element_type=jnp.float32).astype(
            jnp.bfloat16
        ),
        "smp",
        scatter_dimension=1,
        tiled=True,
    ).astype(jnp.float32)
    gram_cross = summed_on_arrival(
        lax.dot_general(added_columns, old_all, contract, preferred_element_type=jnp.float32),
        "smp",
        1,
    )
    fit_old = summed_on_arrival(
        lax.dot_general(target, old_all, contract, preferred_element_type=jnp.float32), "smp", 1
    )
    right_side = jnp.concatenate([new_all, target], axis=1)
    small_gram = taken_together(
        lax.dot_general(added_columns, right_side, contract, preferred_element_type=jnp.float32),
        "smp",
    )
    gram_new = small_gram[:, :-1]
    fit_new = small_gram[:, -1]
    return (
        level0_predictions,
        (gram_old / sample_total)[None],
        (gram_cross / sample_total)[None],
        (gram_new / sample_total)[None],
        fit_old / sample_total,
        (fit_new / sample_total)[None],
    )


def solution(mesh):
    placed = (
        P("smp", ("grp", "blk")),
        P(("grp", "blk"), None, None),
        P(("grp", "blk"), None),
        P(),
        P("smp", ("grp", "pen")),
        P("smp"),
        P(("grp", "pen"), "smp", "blk"),
    )
    return jax.shard_map(
        per_device,
        mesh=mesh,
        in_specs=placed,
        out_specs=(
            P("smp", ("grp", "blk"), None, "pen"),
            P(("grp", "pen"), "blk", "smp"),
            P(("grp", "pen"), "blk", "smp"),
            P(("grp", "pen"), "blk", None),
            P(("grp", "pen"), "smp"),
            P(("grp", "pen"), "blk"),
        ),
        check_vma=False,
    )
```

profile of v0, /device:TPU:36, one launch (start us, length us, event | category | flops | bytes accessed | tf_op | source)
XLA Modules:
  0.0 464.2 jit_solution(8294659211725884553)
XLA Ops:
  7.3 1.7 convolution_convert_fusion.1
  9.0 1.5 convolution_convert_fusion.2
  11.3 1.1 pad_maximum_fusion
  12.7 288.3 %all-reduce.2.cloned.1.call-done = f32[2,512,256]{2,1,0:T(8,128)} async-done(((f32[2,512,256]{2,1,0:T(8,128)}), f32[2,512,256]{2,1,0:T(8,128)}) %all-reduce.2.cloned.1.call-update) | async-done | bytes 1048592 | tf_op jit(solution)/shard_map/psum | solution.py:98
  301.0 1.3 fusion.28
  307.0 16.0 %all_to_all.20 = bf16[4,512,392]{1,2,0:T(8,128)(2,1)S(1)} all-to-all(bf16[4,512,392]{1,2,0:T(8,128)(2,1)S(1)} %broadcast_in_dim.8), channel_id=1, replica_groups=mesh['grp'=2,'smp'=32,'blk'=4,'pen'=2] {'blk'}, dimensions={0} | all-to-all | bytes 3211264 | tf_op jit(solution)/shard_map/all_to_all | solution.py:17
  323.2 0.8 copy-done.2
  324.1 2.0 fusion
  326.2 1.8 pad_maximum_fusion.1
  328.0 1.5 convolution_bitcast_fusion.3
  329.4 13.8 %all-to-all-start.3 = ((f32[32,1,48]{2,1,0:T(1,128)}), f32[32,1,48]{2,1,0:T(1,128)S(1)}, u32[]{:S(2)}, u32[]{:S(2)}) async-start(f32[32,1,48]{2,1,0:T(1,128)} %convolution_bitcast_fusion.3), calls=%async_computation.4 | async-start | bytes 32768 | tf_op jit(solution)/shard_map/all_to_all | solution.py:33
  343.4 0.8 reshape.196
  344.2 20.8 %all-to-all-done.3 = f32[32,1,48]{2,1,0:T(1,128)S(1)} async-done(((f32[32,1,48]{2,1,0:T(1,128)}), f32[32,1,48]{2,1,0:T(1,128)S(1)}, u32[]{:S(2)}, u32[]{:S(2)}) %all-to-all-start.3) | async-done | bytes 6176 | tf_op jit(solution)/shard_map/all_to_all | solution.py:33
  365.0 4.8 %all-to-all-start.2 = ((f32[32,1,264]{2,1,0:T(1,128)}), f32[32,1,264]{2,1,0:T(1,128)S(1)}, u32[]{:S(2)}, u32[]{:S(2)}) async-start(f32[32,1,264]{2,1,0:T(1,128)} %reshape.196), calls=%async_computation.3 | async-start | bytes 98304 | tf_op jit(solution)/shard_map/all_to_all | solution.py:17
  369.7 0.8 convolution_bitcast_fusion.2
  370.6 0.8 reshape.194
  371.4 21.3 %all-to-all-done.2 = f32[32,1,264]{2,1,0:T(1,128)S(1)} async-done(((f32[32,1,264]{2,1,0:T(1,128)}), f32[32,1,264]{2,1,0:T(1,128)S(1)}, u32[]{:S(2)}, u32[]{:S(2)}) %all-to-all-start.2) | async-done | bytes 33824 | tf_op jit(solution)/shard_map/all_to_all | solution.py:17
  392.7 5.4 %all-to-all-start.1 = ((f32[32,1,384]{2,1,0:T(1,128)}), f32[32,1,384]{2,1,0:T(1,128)S(1)}, u32[]{:S(2)}, u32[]{:S(2)}) async-start(f32[32,1,384]{2,1,0:T(1,128)} %reshape.194), calls=%async_computation.2 | async-start | bytes 98304 | tf_op jit(solution)/shard_map/all_to_all | solution.py:33
  399.1 0.8 reduce.7
  400.0 0.7 multiply_reduce_fusion
  401.3 20.2 %all-to-all-done.1 = f32[32,1,384]{2,1,0:T(1,128)S(1)} async-done(((f32[32,1,384]{2,1,0:T(1,128)}), f32[32,1,384]{2,1,0:T(1,128)S(1)}, u32[]{:S(2)}, u32[]{:S(2)}) %all-to-all-start.1) | async-done | bytes 49184 | tf_op jit(solution)/shard_map/all_to_all | solution.py:33
  421.5 0.8 reduce.6
  423.0 32.9 %reduce-scatter.2.cloned.1.call-done = bf16[384,48]{0,1:T(8,128)(2,1)} async-done(((bf16[384,1536]{0,1:T(8,128)(2,1)}), bf16[384,48]{0,1:T(8,128)(2,1)}) %reduce-scatter.2.cloned.1.call-update) | async-done | bytes 36880 | tf_op jit(solution)/shard_map/reduce_scatter | solution.py:124
  456.0 1.4 multiply_bitcast_fusion
  (64 shorter events, 8.5 us)
Async XLA Ops:
  7.2 1.8 copy-start.7
  7.2 3.3 copy-start.5
  7.2 3.3 copy-start.3
  7.2 293.8 %all-reduce.2.cloned.1.call-start = ((), (), s32[]{:S(2)}) async-start(), calls=%async_computation.5 | async-start | bytes 2097152 | tf_op jit(solution)/shard_map/psum | solution.py:98
  11.3 1.3 copy-start.4
  11.3 1.3 copy-start.6
  12.5 443.5 %reduce-scatter.2.cloned.1.call-start = ((), (), s32[]{:S(2)}) async-start(), calls=%async_computation.6 | async-start | bytes 1216512 | tf_op jit(solution)/shard_map/reduce_scatter | solution.py:124
  305.7 1.0 copy-start.1
  306.4 16.7 %copy-start = (bf16[512,256]{0,1:T(8,128)(2,1)}, bf16[512,256]{0,1:T(8,128)(2,1)S(1)}, u32[]{:S(2)}) copy-start(bf16[512,256]{0,1:T(8,128)(2,1)S(1)} %fusion.8) | copy-start | bytes 786436
  323.1 1.0 copy-start.2
  329.4 35.6 %all-to-all-start.3 = ((f32[32,1,48]{2,1,0:T(1,128)}), f32[32,1,48]{2,1,0:T(1,128)S(1)}, u32[]{:S(2)}, u32[]{:S(2)}) async-start(f32[32,1,48]{2,1,0:T(1,128)} %convolution_bitcast_fusion.3), calls=%async_computation.4 | async-start | bytes 32768 | tf_op jit(solution)/shard_map/all_to_all | solution.py:33
  365.0 27.7 %all-to-all-start.2 = ((f32[32,1,264]{2,1,0:T(1,128)}), f32[32,1,264]{2,1,0:T(1,128)S(1)}, u32[]{:S(2)}, u32[]{:S(2)}) async-start(f32[32,1,264]{2,1,0:T(1,128)} %reshape.196), calls=%async_computation.3 | async-start | bytes 98304 | tf_op jit(solution)/shard_map/all_to_all | solution.py:17
  392.7 28.9 %all-to-all-start.1 = ((f32[32,1,384]{2,1,0:T(1,128)}), f32[32,1,384]{2,1,0:T(1,128)S(1)}, u32[]{:S(2)}, u32[]{:S(2)}) async-start(f32[32,1,384]{2,1,0:T(1,128)} %reshape.194), calls=%async_computation.2 | async-start | bytes 98304 | tf_op jit(solution)/shard_map/all_to_all | solution.py:33
Sparse Core Ops, SparseCore 0:
  12.6 288.3 all-reduce.1
  326.3 129.6 reduce-scatter.1
where the time goes:
time: 465 us; the launch traced here: 464 us
  waiting for transfers between devices  384 us (83%)
  starting transfers between devices  24.1 us (5%)
  blocking collectives  16 us (3%)
  between operations  14.5 us (3%)
  matrix products  11 us (2%)
  other arithmetic  9.28 us (2%)
  local copies, waits for them, and re-layouts  5.69 us (1%)
    psum x1, waiting for transfers between devices, per_device(): summed = lax.psum(jnp.stack(local_list), 'smp')  288 us
    all_to_all x2, waiting for transfers between devices, summed_on_arrival(): lax.all_to_all(blocks, axis, split_axis=0, concat_axis=0, tiled=True)  41 us
    reduce_scatter x1, waiting for transfers between devices, per_device(): lax.psum_scatter(lax.dot_general(old_cols, old_all, contract, preferred_e...  32.9 us
    all_to_all x1, waiting for transfers between devices, copy_for_each(): lax.all_to_all(jnp.broadcast_to(shard[None], (count, *shard.shape)), axis...  21.3 us
    all_to_all x2, starting transfers between devices, summed_on_arrival(): lax.all_to_all(blocks, axis, split_axis=0, concat_axis=0, tiled=True)  19.2 us
    all_to_all x1, blocking collectives, copy_for_each(): lax.all_to_all(jnp.broadcast_to(shard[None], (count, *shard.shape)), axis...  16 us
  transfers between devices with their start and end apart: 5, of which 5 were waited for; matrix products, arithmetic and copies ran while one was open for 2% of the time, Pallas kernels for 0%

commit v1 on v0

v1 whole, which is shorter than its diff:
```python
import jax
import jax.numpy as jnp
from jax import lax
from jax.sharding import Mesh, PartitionSpec as P


FOLDS = 4
NEAR = 4
LANES = 128

BF = jnp.bfloat16
F32 = jnp.float32


def exchange(blocks, axis):
    return lax.all_to_all(blocks, axis, split_axis=0, concat_axis=0, tiled=True)


def copies(block, count):
    return jnp.broadcast_to(block[None], (count, *block.shape))


def dot(left, right, dims):
    return lax.dot_general(left, right, (dims, ((), ())), preferred_element_type=F32)


def total(blocks):
    return jnp.sum(blocks.astype(F32), axis=0)


def per_device(
    allele_matrix,
    orthonormal_frames,
    segment_variances,
    lambda_grid,
    trait_levels,
    partition_labels,
    preceding_fits,
):
    row_count = allele_matrix.shape[0]
    block_count, var_width = orthonormal_frames.shape[:2]
    prot_width = trait_levels.shape[1]
    grid_size = lambda_grid.shape[0]
    near, far, blocks = (lax.axis_size(n) for n in ("near", "far", "blk"))
    samples = ("far", "near")
    inverse = 1.0 / float(row_count * near * far)

    old_cols = preceding_fits[0]
    old_all = exchange(copies(old_cols, blocks), "blk")
    rotated = [
        jnp.dot(
            allele_matrix[:, b * var_width : (b + 1) * var_width],
            orthonormal_frames[b],
            preferred_element_type=F32,
        ).astype(BF)
        for b in range(block_count)
    ]
    member = jnp.arange(FOLDS, dtype=jnp.int32)[:, None] == partition_labels[None, :]
    mask = member.astype(F32)
    traits = trait_levels.T
    masked = member.astype(BF)[:, None, :] * traits[None, :, :]
    masked_all = masked.reshape(FOLDS * prot_width, row_count)
    local = jnp.stack([dot(masked_all, r, ((1,), (0,))).astype(BF) for r in rotated])
    local_q = jnp.stack([dot(masked[:, 0], r, ((1,), (0,))).astype(BF) for r in rotated])

    old_width = old_cols.shape[1]
    share = blocks * old_width // (near * far)
    gram_local = jnp.concatenate(
        [dot(old_all[i], old_cols, ((0,), (0,))).astype(BF) for i in range(blocks)]
    )
    gram_local = gram_local.reshape(far, near, share, old_width)
    gram_local = jnp.moveaxis(gram_local, 1, 0).reshape(near, far * share, old_width)
    gram_near = lax.psum_scatter(gram_local, "near", scatter_dimension=0, tiled=True)
    gram_near = gram_near.reshape(far, share, old_width)
    gram_old = lax.psum_scatter(gram_near, "far", scatter_dimension=0, tiled=True)
    gram_old = gram_old.reshape(share, old_width).T.astype(F32) * inverse

    bulk = local.size // (near * LANES)
    slim = local_q.size // (near * LANES)
    packed = jnp.concatenate(
        [local.reshape(near, bulk, LANES), local_q.reshape(near, slim, LANES)], axis=1
    )
    near_sum = total(exchange(packed, "near")).astype(BF)
    packed = jnp.concatenate(
        [near_sum[:bulk].reshape(far, bulk // far, LANES), copies(near_sum[bulk:], far)], axis=1
    )
    packed = exchange(packed, "far")
    far_sum = total(packed)
    bulk_sum = far_sum[: bulk // far].astype(BF)

    damping = 1.0 / (segment_variances[:, None, :] + lambda_grid[None, :, None])
    slim_all = lax.all_gather(far_sum[bulk // far :], "near", axis=0, tiled=True)
    crossed_q = slim_all.reshape(block_count, FOLDS, var_width)
    remainder_q = jnp.sum(crossed_q, axis=1, keepdims=True) - crossed_q
    coeffs_q = (remainder_q[:, :, None, :] * damping[:, None, :, :]).astype(BF)
    coeffs_q = coeffs_q.reshape(block_count, FOLDS * grid_size, var_width)
    fits_q = [
        dot(coeffs_q[b], rotated[b], ((1,), (1,))).reshape(FOLDS, grid_size, row_count)
        for b in range(block_count)
    ]
    added = jnp.concatenate([jnp.sum(mask[:, None, :] * f, axis=0) for f in fits_q], axis=0)
    added = added.astype(BF)
    new_width = added.shape[0]
    new_all = exchange(copies(added, blocks), "blk").reshape(blocks * new_width, row_count)
    target = traits[:1]
    small = dot(added, jnp.concatenate([new_all, target], axis=0), ((1,), (1,)))
    left = jnp.concatenate([added, target], axis=0)
    cross = jnp.concatenate(
        [dot(left, old_all[i], ((1,), (0,))) for i in range(blocks)], axis=1
    )
    cross = jnp.moveaxis(cross.reshape(new_width + 1, near * far, share), 1, 0)
    cross = cross.reshape(near * far, (new_width + 1) * share)
    final = jnp.concatenate([cross, copies(small.reshape(-1), near * far)], axis=1)
    width = final.shape[1]
    final = jnp.pad(final, ((0, 0), (0, -width % LANES)))
    final = exchange(final, samples)
    final = jnp.sum(final, axis=0) * inverse
    cut = (new_width + 1) * share
    cross_sum = final[:cut].reshape(new_width + 1, share)
    small_sum = final[cut:width].reshape(new_width, blocks * new_width + 1)

    bulk_far = lax.all_gather(bulk_sum, "far", axis=0, tiled=True)
    bulk_all = lax.all_gather(bulk_far, "near", axis=0, tiled=True)
    crossed = bulk_all.reshape(block_count, FOLDS, prot_width, var_width).astype(F32)
    remainder = jnp.sum(crossed, axis=1, keepdims=True) - crossed
    preds = []
    for b in range(block_count):
        running = jnp.zeros((grid_size * prot_width, row_count), F32)
        for k in range(FOLDS):
            coeffs = (remainder[b, k][None] * damping[b][:, None, :]).astype(BF)
            coeffs = coeffs.reshape(grid_size * prot_width, var_width)
            running = running + mask[k][None] * dot(coeffs, rotated[b], ((1,), (1,)))
        preds.append(running.astype(BF).reshape(grid_size, prot_width, row_count))
    level0 = jnp.moveaxis(jnp.stack(preds), 3, 0)
    return (
        level0,
        gram_old[None],
        cross_sum[None, :new_width],
        small_sum[None, :, :-1],
        cross_sum[new_width:],
        small_sum[None, :, -1],
    )


def solution(mesh):
    grp, smp, blk, pen = (mesh.shape[n] for n in ("grp", "smp", "blk", "pen"))
    split = Mesh(
        mesh.devices.reshape(grp, smp // NEAR, NEAR, blk, pen),
        ("grp", "far", "near", "blk", "pen"),
    )
    smp = ("far", "near")
    placed = (
        P(smp, ("grp", "blk")),
        P(("grp", "blk"), None, None),
        P(("grp", "blk"), None),
        P(),
        P(smp, ("grp", "pen")),
        P(smp),
        P(("grp", "pen"), smp, "blk"),
    )
    return jax.shard_map(
        per_device,
        mesh=split,
        in_specs=placed,
        out_specs=(
            P(smp, ("grp", "blk"), None, "pen"),
            P(("grp", "pen"), "blk", smp),
            P(("grp", "pen"), "blk", smp),
            P(("grp", "pen"), "blk", None),
            P(("grp", "pen"), smp),
            P(("grp", "pen"), "blk"),
        ),
        check_vma=False,
    )
```

time: 465 us -> 329 us (0.71)
  the two profiles are of different devices: /device:TPU:36 before, /device:TPU:34 now
where the time goes in v1:
time: 329 us; the launch traced here: 328 us
  waiting for transfers between devices  137 us (42%)
  starting transfers between devices  83.6 us (25%)
  blocking collectives  63.9 us (19%)
  matrix products  15.4 us (5%)
  between operations  14.5 us (4%)
  local copies, waits for them, and re-layouts  8.65 us (3%)
  other arithmetic  5.04 us (2%)
    all_to_all x5, starting transfers between devices, exchange(): return lax.all_to_all(blocks, axis, split_axis=0, concat_axis=0, tiled=True)  83.5 us
    reduce_scatter x1, waiting for transfers between devices, per_device(): lax.psum_scatter(gram_near, 'far', scatter_dimension=0, tiled=True)  69.1 us
    all_gather x1, blocking collectives, per_device(): bulk_far = lax.all_gather(bulk_sum, 'far', axis=0, tiled=True)  35.9 us
    all_to_all x5, waiting for transfers between devices, exchange(): return lax.all_to_all(blocks, axis, split_axis=0, concat_axis=0, tiled=True)  35.6 us
    reduce_scatter x1, waiting for transfers between devices, per_device(): lax.psum_scatter(gram_local, 'near', scatter_dimension=0, tiled=True)  32.1 us
    all_gather x1, blocking collectives, per_device(): bulk_all = lax.all_gather(bulk_far, 'near', axis=0, tiled=True)  14.8 us
    dot_general x23, matrix products, dot(): lax.dot_general(left, right, (dims, ((), ())), preferred_element_type=F32)  14.5 us
    all_gather x1, blocking collectives, per_device(): slim_all = lax.all_gather(far_sum[bulk // far:], 'near', axis=0, tiled=True)  13.3 us
  transfers between devices with their start and end apart: 7, of which 5 were waited for; matrix products, arithmetic and copies ran while one was open for 7% of the time, Pallas kernels for 0%

profile of v1, /device:TPU:34, one launch (start us, length us, event | category | flops | bytes accessed | tf_op | source)
XLA Modules:
  0.0 328.1 jit_solution(17805578307977020385)
XLA Ops:
  7.2 2.3 broadcast_in_dim.18
  9.5 44.9 %all-to-all-start.2 = ((bf16[4,512,384]{2,1,0:T(8,128)(2,1)}), bf16[4,512,384]{2,1,0:T(8,128)(2,1)}, u32[]{:S(2)}, u32[]{:S(2)}) async-start(bf16[4,512,384]{2,1,0:T(8,128)(2,1)} %broadcast_in_dim.18), calls=%async_computation.2 | async-start | bytes 3145728 | tf_op jit(solution)/shard_map/all_to_all | solution.py:16
  57.5 9.2 %all-to-all-done.2 = bf16[4,512,384]{2,1,0:T(8,128)(2,1)} async-done(((bf16[4,512,384]{2,1,0:T(8,128)(2,1)}), bf16[4,512,384]{2,1,0:T(8,128)(2,1)}, u32[]{:S(2)}, u32[]{:S(2)}) %all-to-all-start.2) | async-done | bytes 1572896 | tf_op jit(solution)/shard_map/all_to_all | solution.py:16
  66.7 3.6 %all-to-all-start = ((bf16[4,520,128]{2,1,0:T(8,128)(2,1)}), bf16[4,520,128]{2,1,0:T(8,128)(2,1)S(1)}, u32[]{:S(2)}, u32[]{:S(2)}) async-start(bf16[4,520,128]{2,1,0:T(8,128)(2,1)} %pad_maximum_fusion.1), calls=%async_computation | async-start | bytes 1064960 | tf_op jit(solution)/shard_map/all_to_all | solution.py:16
  70.4 1.4 convolution_convert_fusion.2
  71.8 1.4 convolution_convert_fusion.3
  73.2 1.4 convolution_convert_fusion.4
  74.5 1.4 convolution_convert_fusion.5
  76.1 1.1 copy.20
  77.3 3.3 all-to-all-done
  81.4 16.9 %all-to-all-start.1 = ((bf16[8,72,128]{2,1,0:T(8,128)(2,1)}), bf16[8,72,128]{2,1,0:T(8,128)(2,1)S(1)}, u32[]{:S(2)}, u32[]{:S(2)}) async-start(bf16[8,72,128]{2,1,0:T(8,128)(2,1)} %pad_maximum_fusion.3), calls=%async_computation.1 | async-start | bytes 294912 | tf_op jit(solution)/shard_map/all_to_all | solution.py:16
  98.3 32.1 %reduce-scatter.3.cloned.1.call-done = bf16[1,384,384]{2,1,0:T(8,128)(2,1)} async-done(((bf16[4,384,384]{2,1,0:T(8,128)(2,1)}), bf16[1,384,384]{2,1,0:T(8,128)(2,1)}) %reduce-scatter.3.cloned.1.call-update) | async-done | bytes 294928 | tf_op jit(solution)/shard_map/reduce_scatter | solution.py:73
  130.6 69.1 %reduce-scatter.5.cloned.1.call-done = bf16[1,48,384]{2,1,0:T(8,128)(2,1)} async-done(((bf16[8,48,384]{2,1,0:T(8,128)(2,1)}), bf16[1,48,384]{2,1,0:T(8,128)(2,1)}) %reduce-scatter.5.cloned.1.call-update) | async-done | bytes 36880 | tf_op jit(solution)/shard_map/reduce_scatter | solution.py:75
  199.7 1.4 multiply_bitcast_fusion
  201.2 13.3 %all_gather.11 = f32[32,128]{1,0:T(8,128)S(1)} all-gather(f32[8,128]{1,0:T(8,128)S(1)} %slice.193), channel_id=1, replica_groups=mesh['grp'=2,'far'=8,'near'=4,'blk'=4,'pen'=2] {'near'}, dimensions={0}, use_global_device_ids=true | all-gather | bytes 20480 | tf_op jit(solution)/shard_map/all_gather | solution.py:92
  215.7 4.9 %all-to-all-start.3 = ((bf16[4,8,512]{2,1,0:T(8,128)(2,1)}), bf16[4,8,512]{2,1,0:T(8,128)(2,1)S(1)}, u32[]{:S(2)}, u32[]{:S(2)}) async-start(bf16[4,8,512]{2,1,0:T(8,128)(2,1)} %broadcast_in_dim.20), calls=%async_computation.5 | async-start | bytes 65536 | tf_op jit(solution)/shard_map/all_to_all | solution.py:16
  220.6 35.9 %all_gather.9 = bf16[512,128]{1,0:T(8,128)(2,1)S(1)} all-gather(bf16[64,128]{1,0:T(8,128)(2,1)S(1)} %slice.239), channel_id=1, replica_groups=mesh['grp'=2,'far'=8,'near'=4,'blk'=4,'pen'=2] {'far'}, dimensions={0}, use_global_device_ids=true | all-gather | bytes 147456 | tf_op jit(solution)/shard_map/all_gather | solution.py:122
  256.5 14.8 %all_gather.10 = bf16[2048,128]{1,0:T(8,128)(2,1)S(1)} all-gather(bf16[512,128]{1,0:T(8,128)(2,1)S(1)} %all_gather.9), channel_id=1, replica_groups=mesh['grp'=2,'far'=8,'near'=4,'blk'=4,'pen'=2] {'near'}, dimensions={0}, use_global_device_ids=true | all-gather | bytes 655360 | tf_op jit(solution)/shard_map/all_gather | solution.py:123
  274.1 1.2 fusion.25
  275.2 1.2 fusion.24
  276.4 1.2 fusion.23
  277.6 1.2 fusion.22
  280.2 13.3 %all-to-all-start.4 = ((f32[32,1,768]{2,1,0:T(1,128)}), f32[32,1,768]{2,1,0:T(1,128)S(1)}, u32[]{:S(2)}, u32[]{:S(2)}) async-start(f32[32,1,768]{2,1,0:T(1,128)} %copy.22), calls=%async_computation.6 | async-start | bytes 196608 | tf_op jit(solution)/shard_map/all_to_all | solution.py:16
  295.3 23.2 %all-to-all-done.4 = f32[32,1,768]{2,1,0:T(1,128)S(1)} async-done(((f32[32,1,768]{2,1,0:T(1,128)}), f32[32,1,768]{2,1,0:T(1,128)S(1)}, u32[]{:S(2)}, u32[]{:S(2)}) %all-to-all-start.4) | async-done | bytes 98336 | tf_op jit(solution)/shard_map/all_to_all | solution.py:16
  (88 shorter events, 14.3 us)
Async XLA Ops:
  9.5 44.9 %copy-start.3 = (s32[512]{0:T(512)S(1)}, s32[512]{0:T(512)}, u32[]{:S(2)}) copy-start(s32[512]{0:T(512)} %param.12) | copy-start | bytes 6148
  9.5 44.9 %copy-start.1 = (bf16[512,64]{0,1:T(8,128)(2,1)S(1)}, bf16[512,64]{0,1:T(8,128)(2,1)}, u32[]{:S(2)}) copy-start(bf16[512,64]{0,1:T(8,128)(2,1)} %param.11) | copy-start | bytes 196612
  9.5 44.9 %copy-start.5 = (bf16[2,512,512]{2,1,0:T(8,128)(2,1)S(1)}, bf16[2,512,512]{2,1,0:T(8,128)(2,1)}, u32[]{:S(2)}) copy-start(bf16[2,512,512]{2,1,0:T(8,128)(2,1)} %param.8) | copy-start | bytes 3145732
  9.5 44.9 %copy-start.6 = (bf16[512,1024]{1,0:T(8,128)(2,1)S(1)}, bf16[512,1024]{1,0:T(8,128)(2,1)}, u32[]{:S(2)}) copy-start(bf16[512,1024]{1,0:T(8,128)(2,1)} %param.7) | copy-start | bytes 3145732
  9.5 57.2 %all-to-all-start.2 = ((bf16[4,512,384]{2,1,0:T(8,128)(2,1)}), bf16[4,512,384]{2,1,0:T(8,128)(2,1)}, u32[]{:S(2)}, u32[]{:S(2)}) async-start(bf16[4,512,384]{2,1,0:T(8,128)(2,1)} %broadcast_in_dim.18), calls=%async_computation.2 | async-start | bytes 3145728 | tf_op jit(solution)/shard_map/all_to_all | solution.py:16
  56.4 14.0 %copy-start = (bf16[1,512,384]{2,1,0:T(8,128)(2,1)S(1)}, bf16[1,512,384]{2,1,0:T(8,128)(2,1)}, u32[]{:S(2)}) copy-start(bf16[1,512,384]{2,1,0:T(8,128)(2,1)} %param.13) | copy-start | bytes 1179652
  66.7 13.8 %all-to-all-start = ((bf16[4,520,128]{2,1,0:T(8,128)(2,1)}), bf16[4,520,128]{2,1,0:T(8,128)(2,1)S(1)}, u32[]{:S(2)}, u32[]{:S(2)}) async-start(bf16[4,520,128]{2,1,0:T(8,128)(2,1)} %pad_maximum_fusion.1), calls=%async_computation | async-start | bytes 1064960 | tf_op jit(solution)/shard_map/all_to_all | solution.py:16
  70.3 60.1 %reduce-scatter.3.cloned.1.call-start = ((), (), s32[]{:S(2)}) async-start(), calls=%async_computation.7 | async-start | bytes 1474560 | tf_op jit(solution)/shard_map/reduce_scatter | solution.py:73
  77.2 53.3 %copy-start.2 = (f32[2,512]{1,0:T(2,128)S(1)}, f32[2,512]{1,0:T(2,128)}, u32[]{:S(2)}) copy-start(f32[2,512]{1,0:T(2,128)} %param.9) | copy-start | bytes 12292
  77.2 53.3 %copy-start.4 = (f32[4]{0:T(128)S(1)}, f32[4]{0:T(128)}, u32[]{:S(2)}) copy-start(f32[4]{0:T(128)} %param.10) | copy-start | bytes 52
  81.4 119.8 %all-to-all-start.1 = ((bf16[8,72,128]{2,1,0:T(8,128)(2,1)}), bf16[8,72,128]{2,1,0:T(8,128)(2,1)S(1)}, u32[]{:S(2)}, u32[]{:S(2)}) async-start(bf16[8,72,128]{2,1,0:T(8,128)(2,1)} %pad_maximum_fusion.3), calls=%async_computation.1 | async-start | bytes 294912 | tf_op jit(solution)/shard_map/all_to_all | solution.py:16
  98.2 101.5 %reduce-scatter.5.cloned.1.call-start = ((), (), s32[]{:S(2)}) async-start(), calls=%async_computation.8 | async-start | bytes 331776 | tf_op jit(solution)/shard_map/reduce_scatter | solution.py:75
  215.7 63.5 %all-to-all-start.3 = ((bf16[4,8,512]{2,1,0:T(8,128)(2,1)}), bf16[4,8,512]{2,1,0:T(8,128)(2,1)S(1)}, u32[]{:S(2)}, u32[]{:S(2)}) async-start(bf16[4,8,512]{2,1,0:T(8,128)(2,1)} %broadcast_in_dim.20), calls=%async_computation.5 | async-start | bytes 65536 | tf_op jit(solution)/shard_map/all_to_all | solution.py:16
  280.2 38.3 %all-to-all-start.4 = ((f32[32,1,768]{2,1,0:T(1,128)}), f32[32,1,768]{2,1,0:T(1,128)S(1)}, u32[]{:S(2)}, u32[]{:S(2)}) async-start(f32[32,1,768]{2,1,0:T(1,128)} %copy.22), calls=%async_computation.6 | async-start | bytes 196608 | tf_op jit(solution)/shard_map/all_to_all | solution.py:16
Sparse Core Ops, SparseCore 0:
  77.4 52.9 reduce-scatter.2
  133.2 66.4 reduce-scatter.4

commit v2 on v1

--- a/solution.py
+++ b/solution.py
@@ -1,6 +1,8 @@
 import jax
 import jax.numpy as jnp
 from jax import lax
+from jax.experimental import pallas as pl
+from jax.experimental.pallas import tpu as pltpu
 from jax.sharding import Mesh, PartitionSpec as P
 
 
@@ -10,6 +12,7 @@
 
 BF = jnp.bfloat16
 F32 = jnp.float32
+ROWS = (((0,), (0,)), ((), ()))
 
 
 def exchange(blocks, axis):
@@ -26,6 +29,40 @@
 
 def total(blocks):
     return jnp.sum(blocks.astype(F32), axis=0)
+
+
+def paired_gram(side, old_all, old_cols, near, share):
+    blocks, row_count, width = old_all.shape
+    runs = width // (near * share)
+    half = near // 2
+
+    def kernel(side_ref, one_ref, own_ref, gone_ref, kept_ref):
+        gram = lax.dot_general(
+            one_ref[0], own_ref[...], ROWS, preferred_element_type=F32
+        ).astype(BF)
+        first = side_ref[0] == 0
+        for run in range(runs):
+            for high in range(half):
+                at = (run * near + 2 * high) * share
+                even = gram[at : at + share]
+                odd = gram[at + share : at + 2 * share]
+                gone_ref[high, run] = jnp.where(first, odd, even)
+                kept_ref[high, run] = jnp.where(first, even, odd)
+
+    half_shape = jax.ShapeDtypeStruct((half, blocks * runs, share, width), BF)
+    half_spec = pl.BlockSpec((half, runs, share, width), lambda j: (0, j, 0, 0))
+    return pl.pallas_call(
+        kernel,
+        grid=(blocks,),
+        in_specs=[
+            pl.BlockSpec(memory_space=pltpu.SMEM),
+            pl.BlockSpec((1, row_count, width), lambda j: (j, 0, 0)),
+            pl.BlockSpec((row_count, width), lambda j: (0, 0)),
+        ],
+        out_specs=[half_spec, half_spec],
+        out_shape=[half_shape, half_shape],
+        name="paired_gram",
+    )(side.astype(jnp.int32)[None], old_all, old_cols)
 
 
 def per_device(
@@ -42,11 +79,12 @@
     prot_width = trait_levels.shape[1]
     grid_size = lambda_grid.shape[0]
     near, far, blocks = (lax.axis_size(n) for n in ("near", "far", "blk"))
-    samples = ("far", "near")
     inverse = 1.0 / float(row_count * near * far)
 
     old_cols = preceding_fits[0]
-    old_all = exchange(copies(old_cols, blocks), "blk")
+    old_width = old_cols.shape[1]
+    share = blocks * old_width // (near * far)
+    old_all = lax.all_gather(old_cols, "blk", axis=0)
     rotated = [
         jnp.dot(
             allele_matrix[:, b * var_width : (b + 1) * var_width],
@@ -63,34 +101,39 @@
     local = jnp.stack([dot(masked_all, r, ((1,), (0,))).astype(BF) for r in rotated])
     local_q = jnp.stack([dot(masked[:, 0], r, ((1,), (0,))).astype(BF) for r in rotated])
 
-    old_width = old_cols.shape[1]
-    share = blocks * old_width // (near * far)
-    gram_local = jnp.concatenate(
-        [dot(old_all[i], old_cols, ((0,), (0,))).astype(BF) for i in range(blocks)]
-    )
-    gram_local = gram_local.reshape(far, near, share, old_width)
-    gram_local = jnp.moveaxis(gram_local, 1, 0).reshape(near, far * share, old_width)
-    gram_near = lax.psum_scatter(gram_local, "near", scatter_dimension=0, tiled=True)
-    gram_near = gram_near.reshape(far, share, old_width)
-    gram_old = lax.psum_scatter(gram_near, "far", scatter_dimension=0, tiled=True)
+    seat = lax.axis_index("near").astype(jnp.uint32)
+    low, high = seat & jnp.uint32(1), seat >> jnp.uint32(1)
+    gone, kept = paired_gram(low, old_all, old_cols, near, share)
+    met = lax.ppermute(gone, "near", [(i, i ^ 1) for i in range(near)])
+    halves = (kept.astype(F32) + met.astype(F32)).astype(BF)
+    gone = lax.dynamic_index_in_dim(halves, high ^ jnp.uint32(1), 0, keepdims=False)
+    met = lax.ppermute(gone, "near", [(i, i ^ 2) for i in range(near)])
+    kept = lax.dynamic_index_in_dim(halves, high, 0, keepdims=False)
+    gram_local = (kept.astype(F32) + met.astype(F32)).astype(BF)
+    gram_old = lax.psum_scatter(gram_local, "far", scatter_dimension=0, tiled=True)
     gram_old = gram_old.reshape(share, old_width).T.astype(F32) * inverse
 
-    bulk = local.size // (near * LANES)
-    slim = local_q.size // (near * LANES)
+    bulk = block_count * FOLDS * prot_width // near
+    slim = block_count * FOLDS
     packed = jnp.concatenate(
-        [local.reshape(near, bulk, LANES), local_q.reshape(near, slim, LANES)], axis=1
-    )
-    near_sum = total(exchange(packed, "near")).astype(BF)
+        [
+            local.reshape(near, bulk, var_width),
+            copies(local_q.reshape(slim, var_width), near),
+        ],
+        axis=1,
+    )
+    packed = exchange(packed, "near")
+    near_sum = total(packed).astype(BF)
     packed = jnp.concatenate(
-        [near_sum[:bulk].reshape(far, bulk // far, LANES), copies(near_sum[bulk:], far)], axis=1
+        [near_sum[:bulk].reshape(far, bulk // far, var_width), copies(near_sum[bulk:], far)],
+        axis=1,
     )
     packed = exchange(packed, "far")
     far_sum = total(packed)
     bulk_sum = far_sum[: bulk // far].astype(BF)
 
     damping = 1.0 / (segment_variances[:, None, :] + lambda_grid[None, :, None])
-    slim_all = lax.all_gather(far_sum[bulk // far :], "near", axis=0, tiled=True)
-    crossed_q = slim_all.reshape(block_count, FOLDS, var_width)
+    crossed_q = far_sum[bulk // far :].reshape(block_count, FOLDS, var_width)
     remainder_q = jnp.sum(crossed_q, axis=1, keepdims=True) - crossed_q
     coeffs_q = (remainder_q[:, :, None, :] * damping[:, None, :, :]).astype(BF)
     coeffs_q = coeffs_q.reshape(block_count, FOLDS * grid_size, var_width)
@@ -105,22 +148,29 @@
     target = traits[:1]
     small = dot(added, jnp.concatenate([new_all, target], axis=0), ((1,), (1,)))
     left = jnp.concatenate([added, target], axis=0)
-    cross = jnp.concatenate(
-        [dot(left, old_all[i], ((1,), (0,))) for i in range(blocks)], axis=1
-    )
-    cross = jnp.moveaxis(cross.reshape(new_width + 1, near * far, share), 1, 0)
-    cross = cross.reshape(near * far, (new_width + 1) * share)
-    final = jnp.concatenate([cross, copies(small.reshape(-1), near * far)], axis=1)
-    width = final.shape[1]
-    final = jnp.pad(final, ((0, 0), (0, -width % LANES)))
-    final = exchange(final, samples)
-    final = jnp.sum(final, axis=0) * inverse
+    cross = jnp.stack([dot(left, old_all[i], ((1,), (0,))) for i in range(blocks)])
+    cross = cross.reshape(blocks, new_width + 1, far // blocks, near, share)
+    cross = jnp.transpose(cross, (3, 0, 2, 1, 4)).reshape(near, far * (new_width + 1) * share)
+    sums = jnp.concatenate([cross, copies(small.reshape(-1), near)], axis=1)
+    width = sums.shape[1]
+    sums = jnp.pad(sums, ((0, 0), (0, -width % (8 * LANES)))).reshape(near, -1, LANES)
+    sums = total(exchange(sums, "near")).reshape(-1)
     cut = (new_width + 1) * share
+    sums = jnp.concatenate(
+        [sums[: far * cut].reshape(far, cut), copies(sums[far * cut : width], far)], axis=1
+    )
+    width = sums.shape[1]
+    sums = jnp.pad(sums, ((0, 0), (0, -width % (8 * LANES)))).reshape(far, -1, LANES)
+    bulk_rows = bulk_sum.size // LANES
+    packed = jnp.concatenate(
+        [copies(bulk_sum.reshape(bulk_rows, LANES), far), sums.astype(BF)], axis=1
+    )
+    packed = exchange(packed, "far")
+    bulk_far = packed[:, :bulk_rows].reshape(bulk, var_width)
+    bulk_all = exchange(copies(bulk_far, near), "near")
+    final = (total(packed[:, bulk_rows:]) * inverse).reshape(-1)
     cross_sum = final[:cut].reshape(new_width + 1, share)
     small_sum = final[cut:width].reshape(new_width, blocks * new_width + 1)
-
-    bulk_far = lax.all_gather(bulk_sum, "far", axis=0, tiled=True)
-    bulk_all = lax.all_gather(bulk_far, "near", axis=0, tiled=True)
     crossed = bulk_all.reshape(block_count, FOLDS, prot_width, var_width).astype(F32)
     remainder = jnp.sum(crossed, axis=1, keepdims=True) - crossed
     preds = []

time: 329 us -> 267 us (0.81)
  blocking collectives: 63.9 us -> 0 us
  waiting for transfers between devices: 137 us -> 151 us
  starting transfers between devices: 83.6 us -> 73.6 us
  matrix products: 15.4 us -> 8.7 us
  Pallas kernels: 0 us -> 4.42 us
    all_gather x3 -> x0, blocking collectives: 63.9 us -> none  [the longest x1 35.9 us: per_device(): bulk_far = lax.all_gather(bulk_sum, 'far', axis=0, tiled=True)]
    reduce_scatter x2 -> x1, waiting for transfers between devices: 101 us -> 59 us  [per_device(): lax.psum_scatter(gram_local, 'far', scatter_dimension=0, tiled=True)]
    all_to_all x5 -> x6, waiting for transfers between devices: 35.6 us -> 64.9 us  [exchange(): return lax.all_to_all(blocks, axis, split_axis=0, concat_axis=0, tiled=True)]
    all_to_all x5 -> x6, starting transfers between devices: 83.5 us -> 65.8 us  [exchange(): return lax.all_to_all(blocks, axis, split_axis=0, concat_axis=0, tiled=True)]
    ppermute x0 -> x2, waiting for transfers between devices: none -> 16.6 us  [the longest x1 16.6 us: per_device(): met = lax.ppermute(gone, 'near', [(i, i ^ 2) for i in range(near)])]
    all_gather x0 -> x1, waiting for transfers between devices: none -> 9.37 us  [per_device(): old_all = lax.all_gather(old_cols, 'blk', axis=0)]
    dot_general x23 -> x19, matrix products: 14.5 us -> 5.47 us  [dot(): lax.dot_general(left, right, (dims, ((), ())), preferred_element_type=F32)]
    ppermute x0 -> x2, starting transfers between devices: none -> 7.83 us  [the longest x1 4.85 us: per_device(): met = lax.ppermute(gone, 'near', [(i, i ^ 2) for i in range(near)])]
  transfers between devices with their start and end apart: 7 -> 10, of which waited for: 5 -> 8; matrix products, arithmetic and copies ran while one was open for 7% -> 4% of each run, Pallas kernels for 0% -> 2%
where the time goes in v2:
time: 267 us; the launch traced here: 266 us
  waiting for transfers between devices  151 us (57%)
  starting transfers between devices  73.6 us (28%)
  between operations  14.6 us (5%)
  matrix products  8.7 us (3%)
  local copies, waits for them, and re-layouts  7.82 us (3%)
  other arithmetic  6.45 us (2%)
  Pallas kernels  4.42 us (2%)
    all_to_all x6, starting transfers between devices, exchange(): return lax.all_to_all(blocks, axis, split_axis=0, concat_axis=0, tiled=True)  65.8 us
    all_to_all x6, waiting for transfers between devices, exchange(): return lax.all_to_all(blocks, axis, split_axis=0, concat_axis=0, tiled=True)  64.9 us
    reduce_scatter x1, waiting for transfers between devices, per_device(): lax.psum_scatter(gram_local, 'far', scatter_dimension=0, tiled=True)  59 us
    ppermute x1, waiting for transfers between devices, per_device(): met = lax.ppermute(gone, 'near', [(i, i ^ 2) for i in range(near)])  16.6 us
    all_gather x1, waiting for transfers between devices, per_device(): old_all = lax.all_gather(old_cols, 'blk', axis=0)  9.37 us
    dot_general x19, matrix products, dot(): lax.dot_general(left, right, (dims, ((), ())), preferred_element_type=F32)  5.47 us
  transfers between devices with their start and end apart: 10, of which 8 were waited for; matrix products, arithmetic and copies ran while one was open for 4% of the time, Pallas kernels for 2%

profile of v2, /device:TPU:34, one launch (start us, length us, event | category | flops | bytes accessed | tf_op | source)
XLA Modules:
  0.0 266.3 jit_solution(17387544413886349511)
XLA Ops:
  7.2 1.7 convolution_convert_fusion.1
  8.9 1.5 convolution_convert_fusion
  11.6 0.9 pad_maximum_fusion
  12.5 8.5 %all-to-all-start = ((bf16[4,136,512]{2,1,0:T(8,128)(2,1)}), bf16[4,136,512]{2,1,0:T(8,128)(2,1)S(1)}, u32[]{:S(2)}, u32[]{:S(2)}) async-start(bf16[4,136,512]{2,1,0:T(8,128)(2,1)} %pad_maximum_fusion), calls=%async_computation | async-start | bytes 1114112 | tf_op jit(solution)/shard_map/all_to_all | solution.py:19
  21.7 14.5 %all-to-all-done = bf16[4,136,512]{2,1,0:T(8,128)(2,1)S(1)} async-done(((bf16[4,136,512]{2,1,0:T(8,128)(2,1)}), bf16[4,136,512]{2,1,0:T(8,128)(2,1)S(1)}, u32[]{:S(2)}, u32[]{:S(2)}) %all-to-all-start) | async-done | bytes 557088 | tf_op jit(solution)/shard_map/all_to_all | solution.py:19
  37.1 40.7 %all-to-all-start.1 = ((bf16[8,24,512]{2,1,0:T(8,128)(2,1)}), bf16[8,24,512]{2,1,0:T(8,128)(2,1)S(1)}, u32[]{:S(2)}, u32[]{:S(2)}) async-start(bf16[8,24,512]{2,1,0:T(8,128)(2,1)} %pad_maximum_fusion.2), calls=%async_computation.1 | async-start | bytes 393216 | tf_op jit(solution)/shard_map/all_to_all | solution.py:19
  77.8 9.4 %all-gather.2.cloned.1.call-done.one_ref = bf16[4,512,384]{2,1,0:T(8,128)(2,1)} async-done(((bf16[1,512,384]{2,1,0:T(8,128)(2,1)}), bf16[4,512,384]{2,1,0:T(8,128)(2,1)}) %all-gather.2.cloned.1.call-update) | async-done | bytes 1572880 | tf_op jit(solution)/shard_map/all_gather | solution.py:87
  87.2 1.5 fusion.39
  89.5 22.0 %all-to-all-done.1 = bf16[8,24,512]{2,1,0:T(8,128)(2,1)S(1)} async-done(((bf16[8,24,512]{2,1,0:T(8,128)(2,1)}), bf16[8,24,512]{2,1,0:T(8,128)(2,1)S(1)}, u32[]{:S(2)}, u32[]{:S(2)}) %all-to-all-start.1) | async-done | bytes 196640 | tf_op jit(solution)/shard_map/all_to_all | solution.py:19
  112.9 5.0 %all-to-all-start.2 = ((bf16[4,8,512]{2,1,0:T(8,128)(2,1)}), bf16[4,8,512]{2,1,0:T(8,128)(2,1)S(1)}, u32[]{:S(2)}, u32[]{:S(2)}) async-start(bf16[4,8,512]{2,1,0:T(8,128)(2,1)} %broadcast_in_dim.35), calls=%async_computation.2 | async-start | bytes 65536 | tf_op jit(solution)/shard_map/all_to_all | solution.py:19
  119.3 2.6 all-to-all-done.2
  122.8 3.4 %all-to-all-start.3 = ((f32[4,32,128]{2,1,0:T(8,128)}), f32[4,32,128]{2,1,0:T(8,128)S(1)}, u32[]{:S(2)}, u32[]{:S(2)}) async-start(f32[4,32,128]{2,1,0:T(8,128)} %bitcast.167), calls=%async_computation.3 | async-start | bytes 131072 | tf_op jit(solution)/shard_map/all_to_all | solution.py:19
  126.2 5.6 %all-to-all-done.3 = f32[4,32,128]{2,1,0:T(8,128)S(1)} async-done(((f32[4,32,128]{2,1,0:T(8,128)}), f32[4,32,128]{2,1,0:T(8,128)S(1)}, u32[]{:S(2)}, u32[]{:S(2)}) %all-to-all-start.3) | async-done | bytes 65568 | tf_op jit(solution)/shard_map/all_to_all | solution.py:19
  132.8 3.6 %all-to-all-start.4 = ((bf16[8,72,128]{2,1,0:T(8,128)(2,1)}), bf16[8,72,128]{2,1,0:T(8,128)(2,1)S(1)}, u32[]{:S(2)}, u32[]{:S(2)}) async-start(bf16[8,72,128]{2,1,0:T(8,128)(2,1)} %pad_maximum_fusion.3), calls=%async_computation.4 | async-start | bytes 294912 | tf_op jit(solution)/shard_map/all_to_all | solution.py:19
  136.4 4.4 %paired_gram.1 = (bf16[2,8,48,384]{3,2,1,0:T(8,128)(2,1)}, bf16[2,8,48,384]{3,2,1,0:T(8,128)(2,1)}) custom-call(s32[1]{0:T(128)} %bitcast.62.side_ref, bf16[4,512,384]{2,1,0:T(8,128)(2,1)} %all-gather.2.cloned.1.call-done.one_ref, bf16[512,384]{1,0:T(8,128)(2,1)} %bitcast.179), custom_call_target="tpu_custom_call" | custom-call | tf_op jit(solution)/shard_map/paired_gram/pallas_call | solution.py:54
  140.8 3.0 %collective-permute-start = (bf16[2,8,48,384]{3,2,1,0:T(8,128)(2,1)}, bf16[2,8,48,384]{3,2,1,0:T(8,128)(2,1)S(1)}, u32[]{:S(2)}, u32[]{:S(2)}) collective-permute-start(bf16[2,8,48,384]{3,2,1,0:T(8,128)(2,1)} %get-tuple-element.9), channel_id=1, source_target_pairs={{0,8},{8,0},{16,24},{24,16},{1,9},{9,1},{17,25},{25,17},{2,10},{10... | collective-permute-start | bytes 1769480 | tf_op jit(solution)/shard_map/ppermute | solution.py:107
  143.8 20.2 %all-to-all-done.4 = bf16[8,72,128]{2,1,0:T(8,128)(2,1)S(1)} async-done(((bf16[8,72,128]{2,1,0:T(8,128)(2,1)}), bf16[8,72,128]{2,1,0:T(8,128)(2,1)S(1)}, u32[]{:S(2)}, u32[]{:S(2)}) %all-to-all-start.4) | async-done | bytes 147488 | tf_op jit(solution)/shard_map/all_to_all | solution.py:19
  164.1 0.8 broadcast_in_dim.80
  164.9 4.6 %all-to-all-start.5 = ((bf16[4,128,512]{2,1,0:T(8,128)(2,1)}), bf16[4,128,512]{2,1,0:T(8,128)(2,1)S(1)}, u32[]{:S(2)}, u32[]{:S(2)}) async-start(bf16[4,128,512]{2,1,0:T(8,128)(2,1)} %broadcast_in_dim.80), calls=%async_computation.5 | async-start | bytes 1048576 | tf_op jit(solution)/shard_map/all_to_all | solution.py:19
  169.8 4.9 %collective-permute-start.1 = (bf16[8,48,384]{2,1,0:T(8,128)(2,1)S(1)}, bf16[8,48,384]{2,1,0:T(8,128)(2,1)S(1)}, u32[]{:S(2)}, u32[]{:S(2)}) collective-permute-start(bf16[8,48,384]{2,1,0:T(8,128)(2,1)S(1)} %dynamic-slice_bitcast_fusion), channel_id=1, source_target_pairs={{0,16},{8,24},{16,0},{24,8},{1,17},{9,25},{17,1},{25,9},{2,18},{10... | collective-permute-start | bytes 884744 | tf_op jit(solution)/shard_map/ppermute | solution.py:110
  174.6 16.6 %collective-permute-done.1 = bf16[8,48,384]{2,1,0:T(8,128)(2,1)S(1)} collective-permute-done((bf16[8,48,384]{2,1,0:T(8,128)(2,1)S(1)}, bf16[8,48,384]{2,1,0:T(8,128)(2,1)S(1)}, u32[]{:S(2)}, u32[]{:S(2)}) %collective-permute-start.1) | collective-permute-done | bytes 294944 | tf_op jit(solution)/shard_map/ppermute | solution.py:110
  192.1 59.0 %reduce-scatter.2.cloned.1.call-done = bf16[1,48,384]{2,1,0:T(8,128)(2,1)} async-done(((bf16[8,48,384]{2,1,0:T(8,128)(2,1)}), bf16[1,48,384]{2,1,0:T(8,128)(2,1)}) %reduce-scatter.2.cloned.1.call-update) | async-done | bytes 36880 | tf_op jit(solution)/shard_map/reduce_scatter | solution.py:113
  251.1 1.4 multiply_bitcast_fusion
  258.6 0.8 maximum_bitcast_fusion
  (102 shorter events, 15.1 us)
Async XLA Ops:
  7.2 1.7 copy-start.5
  8.9 1.5 copy-start.3
  8.9 1.6 copy-start.1
  12.5 23.7 %all-to-all-start = ((bf16[4,136,512]{2,1,0:T(8,128)(2,1)}), bf16[4,136,512]{2,1,0:T(8,128)(2,1)S(1)}, u32[]{:S(2)}, u32[]{:S(2)}) async-start(bf16[4,136,512]{2,1,0:T(8,128)(2,1)} %pad_maximum_fusion), calls=%async_computation | async-start | bytes 1114112 | tf_op jit(solution)/shard_map/all_to_all | solution.py:19
  21.0 66.2 %all-gather.2.cloned.1.call-start = ((), (), s32[]{:S(2)}) async-start(), calls=%async_computation.7 | async-start | bytes 1966080 | tf_op jit(solution)/shard_map/all_gather | solution.py:87
  37.1 74.5 %all-to-all-start.1 = ((bf16[8,24,512]{2,1,0:T(8,128)(2,1)}), bf16[8,24,512]{2,1,0:T(8,128)(2,1)S(1)}, u32[]{:S(2)}, u32[]{:S(2)}) async-start(bf16[8,24,512]{2,1,0:T(8,128)(2,1)} %pad_maximum_fusion.2), calls=%async_computation.1 | async-start | bytes 393216 | tf_op jit(solution)/shard_map/all_to_all | solution.py:19
  88.9 22.7 %copy-start.2 = (f32[2,512]{1,0:T(2,128)S(1)}, f32[2,512]{1,0:T(2,128)}, u32[]{:S(2)}) copy-start(f32[2,512]{1,0:T(2,128)} %param.9) | copy-start | bytes 12292
  88.9 22.7 %copy-start.4 = (f32[4]{0:T(128)S(1)}, f32[4]{0:T(128)}, u32[]{:S(2)}) copy-start(f32[4]{0:T(128)} %param.10) | copy-start | bytes 52
  112.9 9.0 %all-to-all-start.2 = ((bf16[4,8,512]{2,1,0:T(8,128)(2,1)}), bf16[4,8,512]{2,1,0:T(8,128)(2,1)S(1)}, u32[]{:S(2)}, u32[]{:S(2)}) async-start(bf16[4,8,512]{2,1,0:T(8,128)(2,1)} %broadcast_in_dim.35), calls=%async_computation.2 | async-start | bytes 65536 | tf_op jit(solution)/shard_map/all_to_all | solution.py:19
  122.8 9.0 %all-to-all-start.3 = ((f32[4,32,128]{2,1,0:T(8,128)}), f32[4,32,128]{2,1,0:T(8,128)S(1)}, u32[]{:S(2)}, u32[]{:S(2)}) async-start(f32[4,32,128]{2,1,0:T(8,128)} %bitcast.167), calls=%async_computation.3 | async-start | bytes 131072 | tf_op jit(solution)/shard_map/all_to_all | solution.py:19
  132.8 31.2 %all-to-all-start.4 = ((bf16[8,72,128]{2,1,0:T(8,128)(2,1)}), bf16[8,72,128]{2,1,0:T(8,128)(2,1)S(1)}, u32[]{:S(2)}, u32[]{:S(2)}) async-start(bf16[8,72,128]{2,1,0:T(8,128)(2,1)} %pad_maximum_fusion.3), calls=%async_computation.4 | async-start | bytes 294912 | tf_op jit(solution)/shard_map/all_to_all | solution.py:19
  140.8 28.7 %copy-start = (bf16[2,8,48,384]{3,2,1,0:T(8,128)(2,1)S(1)}, bf16[2,8,48,384]{3,2,1,0:T(8,128)(2,1)}, u32[]{:S(2)}) copy-start(bf16[2,8,48,384]{3,2,1,0:T(8,128)(2,1)} %get-tuple-element.8) | copy-start | bytes 1769476
  140.8 28.7 %collective-permute-start = (bf16[2,8,48,384]{3,2,1,0:T(8,128)(2,1)}, bf16[2,8,48,384]{3,2,1,0:T(8,128)(2,1)S(1)}, u32[]{:S(2)}, u32[]{:S(2)}) collective-permute-start(bf16[2,8,48,384]{3,2,1,0:T(8,128)(2,1)} %get-tuple-element.9), channel_id=1, source_target_pairs={{0,8},{8,0},{16,24},{24,16},{1,9},{9,1},{17,25},{25,17},{2,10},{10... | collective-permute-start | bytes 1769480 | tf_op jit(solution)/shard_map/ppermute | solution.py:107
  164.9 90.2 %all-to-all-start.5 = ((bf16[4,128,512]{2,1,0:T(8,128)(2,1)}), bf16[4,128,512]{2,1,0:T(8,128)(2,1)S(1)}, u32[]{:S(2)}, u32[]{:S(2)}) async-start(bf16[4,128,512]{2,1,0:T(8,128)(2,1)} %broadcast_in_dim.80), calls=%async_computation.5 | async-start | bytes 1048576 | tf_op jit(solution)/shard_map/all_to_all | solution.py:19
  169.5 81.6 %reduce-scatter.2.cloned.1.call-start = ((), (), s32[]{:S(2)}) async-start(), calls=%async_computation.8 | async-start | bytes 331776 | tf_op jit(solution)/shard_map/reduce_scatter | solution.py:113
  169.8 21.5 %collective-permute-start.1 = (bf16[8,48,384]{2,1,0:T(8,128)(2,1)S(1)}, bf16[8,48,384]{2,1,0:T(8,128)(2,1)S(1)}, u32[]{:S(2)}, u32[]{:S(2)}) collective-permute-start(bf16[8,48,384]{2,1,0:T(8,128)(2,1)S(1)} %dynamic-slice_bitcast_fusion), channel_id=1, source_target_pairs={{0,16},{8,24},{16,0},{24,8},{1,17},{9,25},{17,1},{25,9},{2,18},{10... | collective-permute-start | bytes 884744 | tf_op jit(solution)/shard_map/ppermute | solution.py:110
Sparse Core Ops, SparseCore 0:
  23.9 63.2 all-gather.1
  192.2 58.8 reduce-scatter.1

commit v3 on v2

--- a/solution.py
+++ b/solution.py
@@ -31,38 +31,49 @@
     return jnp.sum(blocks.astype(F32), axis=0)
 
 
-def paired_gram(side, old_all, old_cols, near, share):
-    blocks, row_count, width = old_all.shape
+def paired_gram(side, spots, olds, near, share):
+    _, width = olds[0].shape
+    blocks = len(olds)
     runs = width // (near * share)
     half = near // 2
 
-    def kernel(side_ref, one_ref, own_ref, gone_ref, kept_ref):
-        gram = lax.dot_general(
-            one_ref[0], own_ref[...], ROWS, preferred_element_type=F32
-        ).astype(BF)
+    def kernel(side_ref, spots_ref, *refs):
+        own_ref, gone_ref, kept_ref = refs[0], refs[-2], refs[-1]
         first = side_ref[0] == 0
-        for run in range(runs):
-            for high in range(half):
-                at = (run * near + 2 * high) * share
-                even = gram[at : at + share]
-                odd = gram[at + share : at + 2 * share]
-                gone_ref[high, run] = jnp.where(first, odd, even)
-                kept_ref[high, run] = jnp.where(first, even, odd)
+        for j in range(blocks):
+            gram = lax.dot_general(
+                refs[j][...], own_ref[...], ROWS, preferred_element_type=F32
+            ).astype(BF)
+            spot = spots_ref[j] * runs
+            for run in range(runs):
+                for high in range(half):
+                    at = (run * near + 2 * high) * share
+                    even = gram[at : at + share]
+                    odd = gram[at + share : at + 2 * share]
+                    gone_ref[high, spot + run] = jnp.where(first, odd, even)
+                    kept_ref[high, spot + run] = jnp.where(first, even, odd)
 
     half_shape = jax.ShapeDtypeStruct((half, blocks * runs, share, width), BF)
-    half_spec = pl.BlockSpec((half, runs, share, width), lambda j: (0, j, 0, 0))
+    smem, vmem = pl.BlockSpec(memory_space=pltpu.SMEM), pl.BlockSpec(memory_space=pltpu.VMEM)
     return pl.pallas_call(
         kernel,
-        grid=(blocks,),
-        in_specs=[
-            pl.BlockSpec(memory_space=pltpu.SMEM),
-            pl.BlockSpec((1, row_count, width), lambda j: (j, 0, 0)),
-            pl.BlockSpec((row_count, width), lambda j: (0, 0)),
-        ],
-        out_specs=[half_spec, half_spec],
+        in_specs=[smem, smem] + [vmem] * blocks,
+        out_specs=[vmem, vmem],
         out_shape=[half_shape, half_shape],
         name="paired_gram",
-    )(side.astype(jnp.int32)[None], old_all, old_cols)
+    )(side.astype(jnp.int32)[None], spots.astype(jnp.int32), *olds)
+
+
+def narrow(block):
+    return jnp.concatenate(
+        [block[..., i : i + LANES] for i in range(0, block.shape[-1], LANES)], axis=-2
+    )
+
+
+def widen(block, rows):
+    return jnp.concatenate(
+        [block[..., i : i + rows, :] for i in range(0, block.shape[-2], rows)], axis=-1
+    )
 
 
 def per_device(
@@ -84,7 +95,16 @@
     old_cols = preceding_fits[0]
     old_width = old_cols.shape[1]
     share = blocks * old_width // (near * far)
-    old_all = lax.all_gather(old_cols, "blk", axis=0)
+    place = lax.axis_index("blk").astype(jnp.uint32)
+    shifts = (0, *sorted(range(1, blocks), key=lambda s: min(s, blocks - s)))
+    olds = [
+        lax.ppermute(old_cols, "blk", [(i, (i + s) % blocks) for i in range(blocks)])
+        if s
+        else old_cols
+        for s in shifts
+    ]
+    back = jnp.array([blocks - s for s in shifts], jnp.uint32)
+    spots = lax.rem(place + back, jnp.full((blocks,), blocks, jnp.uint32))
     rotated = [
         jnp.dot(
             allele_matrix[:, b * var_width : (b + 1) * var_width],
@@ -103,15 +123,13 @@
 
     seat = lax.axis_index("near").astype(jnp.uint32)
     low, high = seat & jnp.uint32(1), seat >> jnp.uint32(1)
-    gone, kept = paired_gram(low, old_all, old_cols, near, share)
+    gone, kept = paired_gram(low, spots, olds, near, share)
     met = lax.ppermute(gone, "near", [(i, i ^ 1) for i in range(near)])
     halves = (kept.astype(F32) + met.astype(F32)).astype(BF)
     gone = lax.dynamic_index_in_dim(halves, high ^ jnp.uint32(1), 0, keepdims=False)
     met = lax.ppermute(gone, "near", [(i, i ^ 2) for i in range(near)])
     kept = lax.dynamic_index_in_dim(halves, high, 0, keepdims=False)
     gram_local = (kept.astype(F32) + met.astype(F32)).astype(BF)
-    gram_old = lax.psum_scatter(gram_local, "far", scatter_dimension=0, tiled=True)
-    gram_old = gram_old.reshape(share, old_width).T.astype(F32) * inverse
 
     bulk = block_count * FOLDS * prot_width // near
     slim = block_count * FOLDS
@@ -148,7 +166,8 @@
     target = traits[:1]
     small = dot(added, jnp.concatenate([new_all, target], axis=0), ((1,), (1,)))
     left = jnp.concatenate([added, target], axis=0)
-    cross = jnp.stack([dot(left, old_all[i], ((1,), (0,))) for i in range(blocks)])
+    turned = [olds[shifts.index(-m % blocks)] for m in range(blocks)]
+    cross = jnp.stack([dot(left, old, ((1,), (0,))) for old in turned])
     cross = cross.reshape(blocks, new_width + 1, far // blocks, near, share)
     cross = jnp.transpose(cross, (3, 0, 2, 1, 4)).reshape(near, far * (new_width + 1) * share)
     sums = jnp.concatenate([cross, copies(small.reshape(-1), near)], axis=1)
@@ -156,19 +175,26 @@
     sums = jnp.pad(sums, ((0, 0), (0, -width % (8 * LANES)))).reshape(near, -1, LANES)
     sums = total(exchange(sums, "near")).reshape(-1)
     cut = (new_width + 1) * share
+    cross = sums[: far * cut].astype(BF).reshape(blocks, far // blocks, cut)
+    cross = lax.dynamic_slice_in_dim(
+        jnp.concatenate([cross, cross]),
+        lax.rem(jnp.uint32(blocks) - place, jnp.uint32(blocks)),
+        blocks,
+        0,
+    )
     sums = jnp.concatenate(
-        [sums[: far * cut].reshape(far, cut), copies(sums[far * cut : width], far)], axis=1
+        [cross.reshape(far, cut), copies(sums[far * cut : width].astype(BF), far)], axis=1
     )
     width = sums.shape[1]
     sums = jnp.pad(sums, ((0, 0), (0, -width % (8 * LANES)))).reshape(far, -1, LANES)
-    bulk_rows = bulk_sum.size // LANES
-    packed = jnp.concatenate(
-        [copies(bulk_sum.reshape(bulk_rows, LANES), far), sums.astype(BF)], axis=1
-    )
+    slab = narrow(bulk_sum)
+    packed = jnp.concatenate([copies(slab, far), sums, narrow(gram_local)], axis=1)
+    mid = slab.shape[0] + sums.shape[1]
     packed = exchange(packed, "far")
-    bulk_far = packed[:, :bulk_rows].reshape(bulk, var_width)
+    bulk_far = widen(packed[:, : slab.shape[0]], bulk_sum.shape[0]).reshape(bulk, var_width)
     bulk_all = exchange(copies(bulk_far, near), "near")
-    final = (total(packed[:, bulk_rows:]) * inverse).reshape(-1)
+    final = (total(packed[:, slab.shape[0] : mid]) * inverse).reshape(-1)
+    gram_old = widen(total(packed[:, mid:]), share).T * inverse
     cross_sum = final[:cut].reshape(new_width + 1, share)
     small_sum = final[cut:width].reshape(new_width, blocks * new_width + 1)
     crossed = bulk_all.reshape(block_count, FOLDS, prot_width, var_width).astype(F32)

time: 267 us -> 237 us (0.89)
  the two profiles are of different devices: /device:TPU:34 before, /device:TPU:40 now
where the time goes in v3:
time: 237 us; the launch traced here: 236 us
  starting transfers between devices  91.8 us (39%)
  waiting for transfers between devices  60.6 us (26%)
  blocking collectives  57 us (24%)
  matrix products  8.33 us (4%)
  local copies, waits for them, and re-layouts  7.66 us (3%)
  other arithmetic  6.03 us (3%)
  Pallas kernels  3.39 us (1%)
    all_to_all x5, starting transfers between devices, exchange(): return lax.all_to_all(blocks, axis, split_axis=0, concat_axis=0, tiled=True)  72 us
    all_to_all x1, blocking collectives, exchange(): return lax.all_to_all(blocks, axis, split_axis=0, concat_axis=0, tiled=True)  57 us
    ppermute x1, waiting for transfers between devices, per_device(): met = lax.ppermute(gone, 'near', [(i, i ^ 2) for i in range(near)])  24.7 us
    all_to_all x5, waiting for transfers between devices, exchange(): return lax.all_to_all(blocks, axis, split_axis=0, concat_axis=0, tiled=True)  23.2 us
    ppermute x3, waiting for transfers between devices, per_device(): lax.ppermute(old_cols, 'blk', [(i, (i + s) % blocks) for i in range(block...  12.7 us
    ppermute x3, starting transfers between devices, per_device(): lax.ppermute(old_cols, 'blk', [(i, (i + s) % blocks) for i in range(block...  11.7 us
    dot_general x19, matrix products, dot(): lax.dot_general(left, right, (dims, ((), ())), preferred_element_type=F32)  5.09 us
  transfers between devices with their start and end apart: 10, of which 8 were waited for; matrix products, arithmetic and copies ran while one was open for 3% of the time, Pallas kernels for 1%

profile of v3, /device:TPU:40, one launch (start us, length us, event | category | flops | bytes accessed | tf_op | source)
XLA Modules:
  0.0 236.1 jit_solution(13439871094063329714)
XLA Ops:
  0.6 1.7 convolution_convert_fusion
  2.4 1.5 convolution_convert_fusion.1
  5.1 0.9 pad_maximum_fusion
  6.0 8.5 %all-to-all-start = ((bf16[4,136,512]{2,1,0:T(8,128)(2,1)}), bf16[4,136,512]{2,1,0:T(8,128)(2,1)S(1)}, u32[]{:S(2)}, u32[]{:S(2)}) async-start(bf16[4,136,512]{2,1,0:T(8,128)(2,1)} %pad_maximum_fusion), calls=%async_computation | async-start | bytes 1114112 | tf_op jit(solution)/shard_map/all_to_all | solution.py:19
  14.5 3.6 %collective-permute-start.2 = (bf16[512,384]{1,0:T(8,128)(2,1)S(1)}, bf16[512,384]{1,0:T(8,128)(2,1)S(1)}, u32[]{:S(2)}, u32[]{:S(2)}) collective-permute-start(bf16[512,384]{1,0:T(8,128)(2,1)S(1)} %bitcast.149), channel_id=1, source_target_pairs={{0,2},{2,4},{4,6},{6,0},{1,3},{3,5},{5,7},{7,1},{8,10},{10,12},{12... | collective-permute-start | bytes 1179656 | tf_op jit(solution)/shard_map/ppermute | solution.py:101
  18.0 4.9 %collective-permute-start.1 = (bf16[512,384]{1,0:T(8,128)(2,1)S(1)}, bf16[512,384]{1,0:T(8,128)(2,1)S(1)}, u32[]{:S(2)}, u32[]{:S(2)}) collective-permute-start(bf16[512,384]{1,0:T(8,128)(2,1)S(1)} %bitcast.150), channel_id=1, source_target_pairs={{0,4},{2,6},{4,0},{6,2},{1,5},{3,7},{5,1},{7,3},{8,12},{10,14},{12... | collective-permute-start | bytes 1179656 | tf_op jit(solution)/shard_map/ppermute | solution.py:101
  23.0 3.2 %collective-permute-start = (bf16[512,384]{1,0:T(8,128)(2,1)S(1)}, bf16[512,384]{1,0:T(8,128)(2,1)S(1)}, u32[]{:S(2)}, u32[]{:S(2)}) collective-permute-start(bf16[512,384]{1,0:T(8,128)(2,1)S(1)} %bitcast.151), channel_id=1, source_target_pairs={{0,6},{2,0},{4,2},{6,4},{1,7},{3,1},{5,3},{7,5},{8,14},{10,8},{12,... | collective-permute-start | bytes 1179656 | tf_op jit(solution)/shard_map/ppermute | solution.py:101
  26.8 1.9 collective-permute-done.2.refs_1_
  28.6 9.4 %collective-permute-done.1.refs_3_ = bf16[512,384]{1,0:T(8,128)(2,1)S(1)} collective-permute-done((bf16[512,384]{1,0:T(8,128)(2,1)S(1)}, bf16[512,384]{1,0:T(8,128)(2,1)S(1)}, u32[]{:S(2)}, u32[]{:S(2)}) %collective-permute-start.1) | collective-permute-done | bytes 393248 | tf_op jit(solution)/shard_map/ppermute | solution.py:101
  38.1 1.4 collective-permute-done.refs_2_
  40.2 3.4 %paired_gram.1 = (bf16[2,8,48,384]{3,2,1,0:T(8,128)(2,1)}, bf16[2,8,48,384]{3,2,1,0:T(8,128)(2,1)}) custom-call(s32[1]{0:T(128)} %bitcast.24.side_ref, s32[4]{0:T(128)} %and_convert_fusion.spots_ref, bf16[512,384]{1,0:T(8,128)(2,1)} %bitcast.148, bf16[512,384]{1,0:T(8,128)(2,1)} %copy-done.2, bf16[512,384]{1,0:T(8,128)(2,1)} %copy-done.4, ...), custom_call_target="tpu_custom_call" | custom-call | tf_op jit(solution)/shard_map/paired_gram/pallas_call | solution.py:58
  43.6 3.8 %collective-permute-start.3 = (bf16[2,8,48,384]{3,2,1,0:T(8,128)(2,1)}, bf16[2,8,48,384]{3,2,1,0:T(8,128)(2,1)S(1)}, u32[]{:S(2)}, u32[]{:S(2)}) collective-permute-start(bf16[2,8,48,384]{3,2,1,0:T(8,128)(2,1)} %get-tuple-element.9), channel_id=1, source_target_pairs={{0,8},{8,0},{16,24},{24,16},{1,9},{9,1},{17,25},{25,17},{2,10},{10... | collective-permute-start | bytes 1769480 | tf_op jit(solution)/shard_map/ppermute | solution.py:127
  48.2 40.7 %all-to-all-start.1 = ((bf16[8,24,512]{2,1,0:T(8,128)(2,1)}), bf16[8,24,512]{2,1,0:T(8,128)(2,1)S(1)}, u32[]{:S(2)}, u32[]{:S(2)}) async-start(bf16[8,24,512]{2,1,0:T(8,128)(2,1)} %pad_maximum_fusion.2), calls=%async_computation.1 | async-start | bytes 393216 | tf_op jit(solution)/shard_map/all_to_all | solution.py:19
  89.8 1.3 add_convert_fusion
  91.1 4.3 %collective-permute-start.4 = (bf16[8,48,384]{2,1,0:T(8,128)(2,1)S(1)}, bf16[8,48,384]{2,1,0:T(8,128)(2,1)S(1)}, u32[]{:S(2)}, u32[]{:S(2)}) collective-permute-start(bf16[8,48,384]{2,1,0:T(8,128)(2,1)S(1)} %dynamic-slice_bitcast_fusion), channel_id=1, source_target_pairs={{0,16},{8,24},{16,0},{24,8},{1,17},{9,25},{17,1},{25,9},{2,18},{10... | collective-permute-start | bytes 884744 | tf_op jit(solution)/shard_map/ppermute | solution.py:130
  95.7 24.7 %collective-permute-done.4 = bf16[8,48,384]{2,1,0:T(8,128)(2,1)S(1)} collective-permute-done((bf16[8,48,384]{2,1,0:T(8,128)(2,1)S(1)}, bf16[8,48,384]{2,1,0:T(8,128)(2,1)S(1)}, u32[]{:S(2)}, u32[]{:S(2)}) %collective-permute-start.4) | collective-permute-done | bytes 294944 | tf_op jit(solution)/shard_map/ppermute | solution.py:130
  120.4 4.0 %all-to-all-done.1 = bf16[8,24,512]{2,1,0:T(8,128)(2,1)S(1)} async-done(((bf16[8,24,512]{2,1,0:T(8,128)(2,1)}), bf16[8,24,512]{2,1,0:T(8,128)(2,1)S(1)}, u32[]{:S(2)}, u32[]{:S(2)}) %all-to-all-start.1) | async-done | bytes 196640 | tf_op jit(solution)/shard_map/all_to_all | solution.py:19
  125.9 5.0 %all-to-all-start.2 = ((bf16[4,8,512]{2,1,0:T(8,128)(2,1)}), bf16[4,8,512]{2,1,0:T(8,128)(2,1)S(1)}, u32[]{:S(2)}, u32[]{:S(2)}) async-start(bf16[4,8,512]{2,1,0:T(8,128)(2,1)} %broadcast_in_dim.32), calls=%async_computation.2 | async-start | bytes 65536 | tf_op jit(solution)/shard_map/all_to_all | solution.py:19
  132.3 4.0 %all-to-all-done.2 = bf16[4,8,512]{2,1,0:T(8,128)(2,1)S(1)} async-done(((bf16[4,8,512]{2,1,0:T(8,128)(2,1)}), bf16[4,8,512]{2,1,0:T(8,128)(2,1)S(1)}, u32[]{:S(2)}, u32[]{:S(2)}) %all-to-all-start.2) | async-done | bytes 32800 | tf_op jit(solution)/shard_map/all_to_all | solution.py:19
  137.2 6.3 %all-to-all-start.3 = ((f32[4,32,128]{2,1,0:T(8,128)}), f32[4,32,128]{2,1,0:T(8,128)S(1)}, u32[]{:S(2)}, u32[]{:S(2)}) async-start(f32[4,32,128]{2,1,0:T(8,128)} %bitcast.140), calls=%async_computation.3 | async-start | bytes 131072 | tf_op jit(solution)/shard_map/all_to_all | solution.py:19
  143.5 5.7 %all-to-all-done.3 = f32[4,32,128]{2,1,0:T(8,128)S(1)} async-done(((f32[4,32,128]{2,1,0:T(8,128)}), f32[4,32,128]{2,1,0:T(8,128)S(1)}, u32[]{:S(2)}, u32[]{:S(2)}) %all-to-all-start.3) | async-done | bytes 65568 | tf_op jit(solution)/shard_map/all_to_all | solution.py:19
  149.7 57.0 %all_to_all.30 = bf16[8,216,128]{2,1,0:T(8,128)(2,1)S(1)} all-to-all(bf16[8,216,128]{2,1,0:T(8,128)(2,1)S(1)} %slice_dynamic-update-slice_fusion), channel_id=1, replica_groups=mesh['grp'=2,'far'=8,'near'=4,'blk'=4,'pen'=2] {'far'}, dimensions={0} | all-to-all | bytes 884736 | tf_op jit(solution)/shard_map/all_to_all | solution.py:19
  207.5 11.5 %all-to-all-start.5 = ((bf16[4,128,512]{2,1,0:T(8,128)(2,1)}), bf16[4,128,512]{2,1,0:T(8,128)(2,1)S(1)}, u32[]{:S(2)}, u32[]{:S(2)}) async-start(bf16[4,128,512]{2,1,0:T(8,128)(2,1)} %broadcast_in_dim.38), calls=%async_computation.5 | async-start | bytes 1048576 | tf_op jit(solution)/shard_map/all_to_all | solution.py:19
  222.4 9.5 %all-to-all-done.5 = bf16[4,128,512]{2,1,0:T(8,128)(2,1)S(1)} async-done(((bf16[4,128,512]{2,1,0:T(8,128)(2,1)}), bf16[4,128,512]{2,1,0:T(8,128)(2,1)S(1)}, u32[]{:S(2)}, u32[]{:S(2)}) %all-to-all-start.5) | async-done | bytes 524320 | tf_op jit(solution)/shard_map/all_to_all | solution.py:19
  (131 shorter events, 16.7 us)
Async XLA Ops:
  0.6 1.7 copy-start.14
  2.4 1.5 copy-start.12
  2.4 1.6 copy-start.10
  5.1 9.4 %copy-start = (bf16[1,512,384]{2,1,0:T(8,128)(2,1)S(1)}, bf16[1,512,384]{2,1,0:T(8,128)(2,1)}, u32[]{:S(2)}) copy-start(bf16[1,512,384]{2,1,0:T(8,128)(2,1)} %param.14) | copy-start | bytes 1179652
  5.1 21.1 %copy-start.15 = (u32[4]{0:T(128)S(1)}, u32[4]{0:T(128)}, u32[]{:S(2)}) copy-start(u32[4]{0:T(128)} %constant.33.clone) | copy-start | bytes 52
  6.0 41.4 %all-to-all-start = ((bf16[4,136,512]{2,1,0:T(8,128)(2,1)}), bf16[4,136,512]{2,1,0:T(8,128)(2,1)S(1)}, u32[]{:S(2)}, u32[]{:S(2)}) async-start(bf16[4,136,512]{2,1,0:T(8,128)(2,1)} %pad_maximum_fusion), calls=%async_computation | async-start | bytes 1114112 | tf_op jit(solution)/shard_map/all_to_all | solution.py:19
  14.5 14.2 %collective-permute-start.2 = (bf16[512,384]{1,0:T(8,128)(2,1)S(1)}, bf16[512,384]{1,0:T(8,128)(2,1)S(1)}, u32[]{:S(2)}, u32[]{:S(2)}) collective-permute-start(bf16[512,384]{1,0:T(8,128)(2,1)S(1)} %bitcast.149), channel_id=1, source_target_pairs={{0,2},{2,4},{4,6},{6,0},{1,3},{3,5},{5,7},{7,1},{8,10},{10,12},{12... | collective-permute-start | bytes 1179656 | tf_op jit(solution)/shard_map/ppermute | solution.py:101
  18.0 20.0 %collective-permute-start.1 = (bf16[512,384]{1,0:T(8,128)(2,1)S(1)}, bf16[512,384]{1,0:T(8,128)(2,1)S(1)}, u32[]{:S(2)}, u32[]{:S(2)}) collective-permute-start(bf16[512,384]{1,0:T(8,128)(2,1)S(1)} %bitcast.150), channel_id=1, source_target_pairs={{0,4},{2,6},{4,0},{6,2},{1,5},{3,7},{5,1},{7,3},{8,12},{10,14},{12... | collective-permute-start | bytes 1179656 | tf_op jit(solution)/shard_map/ppermute | solution.py:101
  23.0 16.5 %collective-permute-start = (bf16[512,384]{1,0:T(8,128)(2,1)S(1)}, bf16[512,384]{1,0:T(8,128)(2,1)S(1)}, u32[]{:S(2)}, u32[]{:S(2)}) collective-permute-start(bf16[512,384]{1,0:T(8,128)(2,1)S(1)} %bitcast.151), channel_id=1, source_target_pairs={{0,6},{2,0},{4,2},{6,4},{1,7},{3,1},{5,3},{7,5},{8,14},{10,8},{12,... | collective-permute-start | bytes 1179656 | tf_op jit(solution)/shard_map/ppermute | solution.py:101
  28.6 10.8 %copy-start.2 = (bf16[512,384]{1,0:T(8,128)(2,1)}, bf16[512,384]{1,0:T(8,128)(2,1)S(1)}, u32[]{:S(2)}) copy-start(bf16[512,384]{1,0:T(8,128)(2,1)S(1)} %collective-permute-done.2.refs_1_) | copy-start | bytes 1179652
  38.1 1.4 copy-start.6
  43.6 46.2 %copy-start.8 = (bf16[2,8,48,384]{3,2,1,0:T(8,128)(2,1)S(1)}, bf16[2,8,48,384]{3,2,1,0:T(8,128)(2,1)}, u32[]{:S(2)}) copy-start(bf16[2,8,48,384]{3,2,1,0:T(8,128)(2,1)} %get-tuple-element.8) | copy-start | bytes 1769476
  43.6 45.4 %collective-permute-start.3 = (bf16[2,8,48,384]{3,2,1,0:T(8,128)(2,1)}, bf16[2,8,48,384]{3,2,1,0:T(8,128)(2,1)S(1)}, u32[]{:S(2)}, u32[]{:S(2)}) collective-permute-start(bf16[2,8,48,384]{3,2,1,0:T(8,128)(2,1)} %get-tuple-element.9), channel_id=1, source_target_pairs={{0,8},{8,0},{16,24},{24,16},{1,9},{9,1},{17,25},{25,17},{2,10},{10... | collective-permute-start | bytes 1769480 | tf_op jit(solution)/shard_map/ppermute | solution.py:127
  48.2 76.2 %all-to-all-start.1 = ((bf16[8,24,512]{2,1,0:T(8,128)(2,1)}), bf16[8,24,512]{2,1,0:T(8,128)(2,1)S(1)}, u32[]{:S(2)}, u32[]{:S(2)}) async-start(bf16[8,24,512]{2,1,0:T(8,128)(2,1)} %pad_maximum_fusion.2), calls=%async_computation.1 | async-start | bytes 393216 | tf_op jit(solution)/shard_map/all_to_all | solution.py:19
  89.8 5.7 %copy-start.1 = (bf16[1,512,384]{2,1,0:T(8,128)(2,1)S(1)}, bf16[1,512,384]{2,1,0:T(8,128)(2,1)}, u32[]{:S(2)}) copy-start(bf16[1,512,384]{2,1,0:T(8,128)(2,1)} %param.14) | copy-start | bytes 1179652
  91.1 33.4 %copy-start.11 = (f32[2,512]{1,0:T(2,128)S(1)}, f32[2,512]{1,0:T(2,128)}, u32[]{:S(2)}) copy-start(f32[2,512]{1,0:T(2,128)} %param.10) | copy-start | bytes 12292
  91.1 33.4 %copy-start.13 = (f32[4]{0:T(128)S(1)}, f32[4]{0:T(128)}, u32[]{:S(2)}) copy-start(f32[4]{0:T(128)} %param.11) | copy-start | bytes 52
  91.1 29.2 %collective-permute-start.4 = (bf16[8,48,384]{2,1,0:T(8,128)(2,1)S(1)}, bf16[8,48,384]{2,1,0:T(8,128)(2,1)S(1)}, u32[]{:S(2)}, u32[]{:S(2)}) collective-permute-start(bf16[8,48,384]{2,1,0:T(8,128)(2,1)S(1)} %dynamic-slice_bitcast_fusion), channel_id=1, source_target_pairs={{0,16},{8,24},{16,0},{24,8},{1,17},{9,25},{17,1},{25,9},{2,18},{10... | collective-permute-start | bytes 884744 | tf_op jit(solution)/shard_map/ppermute | solution.py:130
  120.4 10.7 %copy-start.7 = (bf16[512,384]{1,0:T(8,128)(2,1)S(1)}, bf16[512,384]{1,0:T(8,128)(2,1)}, u32[]{:S(2)}) copy-start(bf16[512,384]{1,0:T(8,128)(2,1)} %copy-done.6) | copy-start | bytes 1179652
  124.7 6.7 %copy-start.3 = (bf16[512,384]{1,0:T(8,128)(2,1)S(1)}, bf16[512,384]{1,0:T(8,128)(2,1)}, u32[]{:S(2)}) copy-start(bf16[512,384]{1,0:T(8,128)(2,1)} %copy-done.2) | copy-start | bytes 1179652
  125.0 6.8 %copy-start.5 = (bf16[512,384]{1,0:T(8,128)(2,1)S(1)}, bf16[512,384]{1,0:T(8,128)(2,1)}, u32[]{:S(2)}) copy-start(bf16[512,384]{1,0:T(8,128)(2,1)} %copy-done.4) | copy-start | bytes 1179652
  125.9 10.4 %all-to-all-start.2 = ((bf16[4,8,512]{2,1,0:T(8,128)(2,1)}), bf16[4,8,512]{2,1,0:T(8,128)(2,1)S(1)}, u32[]{:S(2)}, u32[]{:S(2)}) async-start(bf16[4,8,512]{2,1,0:T(8,128)(2,1)} %broadcast_in_dim.32), calls=%async_computation.2 | async-start | bytes 65536 | tf_op jit(solution)/shard_map/all_to_all | solution.py:19
  137.2 12.1 %all-to-all-start.3 = ((f32[4,32,128]{2,1,0:T(8,128)}), f32[4,32,128]{2,1,0:T(8,128)S(1)}, u32[]{:S(2)}, u32[]{:S(2)}) async-start(f32[4,32,128]{2,1,0:T(8,128)} %bitcast.140), calls=%async_computation.3 | async-start | bytes 131072 | tf_op jit(solution)/shard_map/all_to_all | solution.py:19
  207.5 24.3 %all-to-all-start.5 = ((bf16[4,128,512]{2,1,0:T(8,128)(2,1)}), bf16[4,128,512]{2,1,0:T(8,128)(2,1)S(1)}, u32[]{:S(2)}, u32[]{:S(2)}) async-start(bf16[4,128,512]{2,1,0:T(8,128)(2,1)} %broadcast_in_dim.38), calls=%async_computation.5 | async-start | bytes 1048576 | tf_op jit(solution)/shard_map/all_to_all | solution.py:19
  (2 other events, 1.6 us)

commit v4 on v3

--- a/solution.py
+++ b/solution.py
@@ -89,7 +89,9 @@
     block_count, var_width = orthonormal_frames.shape[:2]
     prot_width = trait_levels.shape[1]
     grid_size = lambda_grid.shape[0]
-    near, far, blocks = (lax.axis_size(n) for n in ("near", "far", "blk"))
+    near, wide, blocks = (lax.axis_size(n) for n in ("near", "wide", "blk"))
+    far = wide * lax.axis_size("mid")
+    away = ("wide", "mid")
     inverse = 1.0 / float(row_count * near * far)
 
     old_cols = preceding_fits[0]
@@ -131,6 +133,13 @@
     kept = lax.dynamic_index_in_dim(halves, high, 0, keepdims=False)
     gram_local = (kept.astype(F32) + met.astype(F32)).astype(BF)
 
+    part = lax.axis_index("mid").astype(jnp.uint32)
+    gram_local = gram_local.reshape(wide, far // wide, share, old_width)
+    gone = lax.dynamic_index_in_dim(gram_local, part ^ jnp.uint32(1), 1, keepdims=False)
+    met = lax.ppermute(gone, "mid", [(0, 1), (1, 0)])
+    kept = lax.dynamic_index_in_dim(gram_local, part, 1, keepdims=False)
+    gram_local = (kept.astype(F32) + met.astype(F32)).astype(BF)
+
     bulk = block_count * FOLDS * prot_width // near
     slim = block_count * FOLDS
     packed = jnp.concatenate(
@@ -146,7 +155,7 @@
         [near_sum[:bulk].reshape(far, bulk // far, var_width), copies(near_sum[bulk:], far)],
         axis=1,
     )
-    packed = exchange(packed, "far")
+    packed = exchange(packed, away)
     far_sum = total(packed)
     bulk_sum = far_sum[: bulk // far].astype(BF)
 
@@ -188,13 +197,13 @@
     width = sums.shape[1]
     sums = jnp.pad(sums, ((0, 0), (0, -width % (8 * LANES)))).reshape(far, -1, LANES)
     slab = narrow(bulk_sum)
-    packed = jnp.concatenate([copies(slab, far), sums, narrow(gram_local)], axis=1)
-    mid = slab.shape[0] + sums.shape[1]
-    packed = exchange(packed, "far")
+    packed = jnp.concatenate([copies(slab, far), sums], axis=1)
+    packed = exchange(packed, away)
     bulk_far = widen(packed[:, : slab.shape[0]], bulk_sum.shape[0]).reshape(bulk, var_width)
-    bulk_all = exchange(copies(bulk_far, near), "near")
-    final = (total(packed[:, slab.shape[0] : mid]) * inverse).reshape(-1)
-    gram_old = widen(total(packed[:, mid:]), share).T * inverse
+    bulk_all = lax.all_gather(bulk_far, "near", axis=0, tiled=True)
+    final = (total(packed[:, slab.shape[0] :]) * inverse).reshape(-1)
+    gram_all = exchange(gram_local, "wide")
+    gram_old = total(gram_all).T * inverse
     cross_sum = final[:cut].reshape(new_width + 1, share)
     small_sum = final[cut:width].reshape(new_width, blocks * new_width + 1)
     crossed = bulk_all.reshape(block_count, FOLDS, prot_width, var_width).astype(F32)
@@ -221,10 +230,10 @@
 def solution(mesh):
     grp, smp, blk, pen = (mesh.shape[n] for n in ("grp", "smp", "blk", "pen"))
     split = Mesh(
-        mesh.devices.reshape(grp, smp // NEAR, NEAR, blk, pen),
-        ("grp", "far", "near", "blk", "pen"),
-    )
-    smp = ("far", "near")
+        mesh.devices.reshape(grp, smp // (2 * NEAR), 2, NEAR, blk, pen),
+        ("grp", "wide", "mid", "near", "blk", "pen"),
+    )
+    smp = ("wide", "mid", "near")
     placed = (
         P(smp, ("grp", "blk")),
         P(("grp", "blk"), None, None),

time: 237 us -> 259 us (1.093)
  waiting for transfers between devices: 60.6 us -> 108 us
  blocking collectives: 57 us -> 15.5 us
  starting transfers between devices: 91.8 us -> 106 us
    all_to_all x1 -> x0, blocking collectives: 57 us -> none  [exchange(): return lax.all_to_all(blocks, axis, split_axis=0, concat_axis=0, tiled=True)]
    all_to_all x5 -> x6, waiting for transfers between devices: 23.2 us -> 60.8 us  [exchange(): return lax.all_to_all(blocks, axis, split_axis=0, concat_axis=0, tiled=True)]
    all_gather x0 -> x1, blocking collectives: none -> 15.5 us  [per_device(): bulk_all = lax.all_gather(bulk_far, 'near', axis=0, tiled=True)]
    ppermute x0 -> x1, waiting for transfers between devices: none -> 10.5 us  [per_device(): met = lax.ppermute(gone, 'mid', [(0, 1), (1, 0)])]
    all_to_all x5 -> x6, starting transfers between devices: 72 us -> 81.4 us  [exchange(): return lax.all_to_all(blocks, axis, split_axis=0, concat_axis=0, tiled=True)]
    ppermute x0 -> x1, starting transfers between devices: none -> 5.18 us  [per_device(): met = lax.ppermute(gone, 'mid', [(0, 1), (1, 0)])]
  transfers between devices with their start and end apart: 10 -> 12, of which waited for: 8 -> 9; matrix products, arithmetic and copies ran while one was open for 3% -> 3% of each run, Pallas kernels for 1% -> 1%
where the time goes in v4:
time: 259 us; the launch traced here: 258 us
  waiting for transfers between devices  108 us (42%)
  starting transfers between devices  106 us (41%)
  blocking collectives  15.5 us (6%)
  matrix products  8.33 us (3%)
  local copies, waits for them, and re-layouts  7.46 us (3%)
  other arithmetic  7.43 us (3%)
  Pallas kernels  3.38 us (1%)
    all_to_all x6, starting transfers between devices, exchange(): return lax.all_to_all(blocks, axis, split_axis=0, concat_axis=0, tiled=True)  81.4 us
    all_to_all x6, waiting for transfers between devices, exchange(): return lax.all_to_all(blocks, axis, split_axis=0, concat_axis=0, tiled=True)  60.8 us
    ppermute x1, waiting for transfers between devices, per_device(): met = lax.ppermute(gone, 'near', [(i, i ^ 2) for i in range(near)])  24 us
    all_gather x1, blocking collectives, per_device(): bulk_all = lax.all_gather(bulk_far, 'near', axis=0, tiled=True)  15.5 us
    ppermute x3, waiting for transfers between devices, per_device(): lax.ppermute(old_cols, 'blk', [(i, (i + s) % blocks) for i in range(block...  12.7 us
    ppermute x3, starting transfers between devices, per_device(): lax.ppermute(old_cols, 'blk', [(i, (i + s) % blocks) for i in range(block...  11.7 us
    ppermute x1, waiting for transfers between devices, per_device(): met = lax.ppermute(gone, 'mid', [(0, 1), (1, 0)])  10.5 us
  transfers between devices with their start and end apart: 12, of which 9 were waited for; matrix products, arithmetic and copies ran while one was open for 3% of the time, Pallas kernels for 1%

profile of v4, /device:TPU:40, one launch (start us, length us, event | category | flops | bytes accessed | tf_op | source)
XLA Modules:
  0.0 257.7 jit_solution(751463715875298071)
XLA Ops:
  0.6 1.7 convolution_convert_fusion
  2.4 1.5 convolution_convert_fusion.1
  6.0 8.5 %all-to-all-start = ((bf16[4,136,512]{2,1,0:T(8,128)(2,1)}), bf16[4,136,512]{2,1,0:T(8,128)(2,1)S(1)}, u32[]{:S(2)}, u32[]{:S(2)}) async-start(bf16[4,136,512]{2,1,0:T(8,128)(2,1)} %pad_maximum_fusion), calls=%async_computation | async-start | bytes 1114112 | tf_op jit(solution)/shard_map/all_to_all | solution.py:19
  14.5 3.6 %collective-permute-start.2 = (bf16[512,384]{1,0:T(8,128)(2,1)S(1)}, bf16[512,384]{1,0:T(8,128)(2,1)S(1)}, u32[]{:S(2)}, u32[]{:S(2)}) collective-permute-start(bf16[512,384]{1,0:T(8,128)(2,1)S(1)} %bitcast.156), channel_id=1, source_target_pairs={{0,2},{2,4},{4,6},{6,0},{1,3},{3,5},{5,7},{7,1},{8,10},{10,12},{12... | collective-permute-start | bytes 1179656 | tf_op jit(solution)/shard_map/ppermute | solution.py:103
  18.0 4.9 %collective-permute-start.1 = (bf16[512,384]{1,0:T(8,128)(2,1)S(1)}, bf16[512,384]{1,0:T(8,128)(2,1)S(1)}, u32[]{:S(2)}, u32[]{:S(2)}) collective-permute-start(bf16[512,384]{1,0:T(8,128)(2,1)S(1)} %bitcast.157), channel_id=1, source_target_pairs={{0,4},{2,6},{4,0},{6,2},{1,5},{3,7},{5,1},{7,3},{8,12},{10,14},{12... | collective-permute-start | bytes 1179656 | tf_op jit(solution)/shard_map/ppermute | solution.py:103
  23.0 3.2 %collective-permute-start = (bf16[512,384]{1,0:T(8,128)(2,1)S(1)}, bf16[512,384]{1,0:T(8,128)(2,1)S(1)}, u32[]{:S(2)}, u32[]{:S(2)}) collective-permute-start(bf16[512,384]{1,0:T(8,128)(2,1)S(1)} %bitcast.158), channel_id=1, source_target_pairs={{0,6},{2,0},{4,2},{6,4},{1,7},{3,1},{5,3},{7,5},{8,14},{10,8},{12,... | collective-permute-start | bytes 1179656 | tf_op jit(solution)/shard_map/ppermute | solution.py:103
  26.8 1.9 collective-permute-done.2.refs_1_
  28.6 9.4 %collective-permute-done.1.refs_3_ = bf16[512,384]{1,0:T(8,128)(2,1)S(1)} collective-permute-done((bf16[512,384]{1,0:T(8,128)(2,1)S(1)}, bf16[512,384]{1,0:T(8,128)(2,1)S(1)}, u32[]{:S(2)}, u32[]{:S(2)}) %collective-permute-start.1) | collective-permute-done | bytes 393248 | tf_op jit(solution)/shard_map/ppermute | solution.py:103
  40.2 3.4 %paired_gram.1 = (bf16[2,8,48,384]{3,2,1,0:T(8,128)(2,1)}, bf16[2,8,48,384]{3,2,1,0:T(8,128)(2,1)}) custom-call(s32[1]{0:T(128)} %bitcast.50.side_ref, s32[4]{0:T(128)} %and_convert_fusion.spots_ref, bf16[512,384]{1,0:T(8,128)(2,1)} %bitcast.155, bf16[512,384]{1,0:T(8,128)(2,1)} %copy-done.2, bf16[512,384]{1,0:T(8,128)(2,1)} %copy-done.4, ...), custom_call_target="tpu_custom_call" | custom-call | tf_op jit(solution)/shard_map/paired_gram/pallas_call | solution.py:58
  43.6 3.8 %collective-permute-start.3 = (bf16[2,8,48,384]{3,2,1,0:T(8,128)(2,1)}, bf16[2,8,48,384]{3,2,1,0:T(8,128)(2,1)S(1)}, u32[]{:S(2)}, u32[]{:S(2)}) collective-permute-start(bf16[2,8,48,384]{3,2,1,0:T(8,128)(2,1)} %get-tuple-element.9), channel_id=1, source_target_pairs={{0,8},{8,0},{16,24},{24,16},{1,9},{9,1},{17,25},{25,17},{2,10},{10... | collective-permute-start | bytes 1769480 | tf_op jit(solution)/shard_map/ppermute | solution.py:129
  48.2 40.8 %all-to-all-start.1 = ((bf16[8,24,512]{2,1,0:T(8,128)(2,1)}), bf16[8,24,512]{2,1,0:T(8,128)(2,1)S(1)}, u32[]{:S(2)}, u32[]{:S(2)}) async-start(bf16[8,24,512]{2,1,0:T(8,128)(2,1)} %pad_maximum_fusion.2), calls=%async_computation.1 | async-start | bytes 393216 | tf_op jit(solution)/shard_map/all_to_all | solution.py:19
  91.2 4.3 %collective-permute-start.4 = (bf16[8,48,384]{2,1,0:T(8,128)(2,1)S(1)}, bf16[8,48,384]{2,1,0:T(8,128)(2,1)S(1)}, u32[]{:S(2)}, u32[]{:S(2)}) collective-permute-start(bf16[8,48,384]{2,1,0:T(8,128)(2,1)S(1)} %dynamic-slice_bitcast_fusion), channel_id=1, source_target_pairs={{0,16},{8,24},{16,0},{24,8},{1,17},{9,25},{17,1},{25,9},{2,18},{10... | collective-permute-start | bytes 884744 | tf_op jit(solution)/shard_map/ppermute | solution.py:132
  96.4 24.0 %collective-permute-done.4 = bf16[8,48,384]{2,1,0:T(8,128)(2,1)S(1)} collective-permute-done((bf16[8,48,384]{2,1,0:T(8,128)(2,1)S(1)}, bf16[8,48,384]{2,1,0:T(8,128)(2,1)S(1)}, u32[]{:S(2)}, u32[]{:S(2)}) %collective-permute-start.4) | collective-permute-done | bytes 294944 | tf_op jit(solution)/shard_map/ppermute | solution.py:132
  120.4 4.0 %all-to-all-done.1 = bf16[8,24,512]{2,1,0:T(8,128)(2,1)S(1)} async-done(((bf16[8,24,512]{2,1,0:T(8,128)(2,1)}), bf16[8,24,512]{2,1,0:T(8,128)(2,1)S(1)}, u32[]{:S(2)}, u32[]{:S(2)}) %all-to-all-start.1) | async-done | bytes 196640 | tf_op jit(solution)/shard_map/all_to_all | solution.py:19
  125.9 4.9 %all-to-all-start.2 = ((bf16[4,8,512]{2,1,0:T(8,128)(2,1)}), bf16[4,8,512]{2,1,0:T(8,128)(2,1)S(1)}, u32[]{:S(2)}, u32[]{:S(2)}) async-start(bf16[4,8,512]{2,1,0:T(8,128)(2,1)} %broadcast_in_dim.28), calls=%async_computation.2 | async-start | bytes 65536 | tf_op jit(solution)/shard_map/all_to_all | solution.py:19
  132.2 4.0 %all-to-all-done.2 = bf16[4,8,512]{2,1,0:T(8,128)(2,1)S(1)} async-done(((bf16[4,8,512]{2,1,0:T(8,128)(2,1)}), bf16[4,8,512]{2,1,0:T(8,128)(2,1)S(1)}, u32[]{:S(2)}, u32[]{:S(2)}) %all-to-all-start.2) | async-done | bytes 32800 | tf_op jit(solution)/shard_map/all_to_all | solution.py:19
  137.1 6.4 %all-to-all-start.3 = ((f32[4,32,128]{2,1,0:T(8,128)}), f32[4,32,128]{2,1,0:T(8,128)S(1)}, u32[]{:S(2)}, u32[]{:S(2)}) async-start(f32[4,32,128]{2,1,0:T(8,128)} %bitcast.147), calls=%async_computation.3 | async-start | bytes 131072 | tf_op jit(solution)/shard_map/all_to_all | solution.py:19
  143.5 5.2 %collective-permute-start.5 = (bf16[4,48,384]{2,1,0:T(8,128)(2,1)S(1)}, bf16[4,48,384]{2,1,0:T(8,128)(2,1)S(1)}, u32[]{:S(2)}, u32[]{:S(2)}) collective-permute-start(bf16[4,48,384]{2,1,0:T(8,128)(2,1)S(1)} %dynamic-slice_bitcast_fusion.1), channel_id=1, source_target_pairs={{0,32},{32,0},{1,33},{33,1},{2,34},{34,2},{3,35},{35,3},{4,36},{36... | collective-permute-start | bytes 442376 | tf_op jit(solution)/shard_map/ppermute | solution.py:139
  148.7 10.5 %collective-permute-done.5 = bf16[4,48,384]{2,1,0:T(8,128)(2,1)S(1)} collective-permute-done((bf16[4,48,384]{2,1,0:T(8,128)(2,1)S(1)}, bf16[4,48,384]{2,1,0:T(8,128)(2,1)S(1)}, u32[]{:S(2)}, u32[]{:S(2)}) %collective-permute-start.5) | collective-permute-done | bytes 147488 | tf_op jit(solution)/shard_map/ppermute | solution.py:139
  160.0 16.0 %all-to-all-start.5 = ((bf16[4,48,384]{2,1,0:T(8,128)(2,1)}), bf16[4,48,384]{2,1,0:T(8,128)(2,1)S(1)}, u32[]{:S(2)}, u32[]{:S(2)}) async-start(bf16[4,48,384]{2,1,0:T(8,128)(2,1)} %fusion.23), calls=%async_computation.5 | async-start | bytes 294912 | tf_op jit(solution)/shard_map/all_to_all | solution.py:19
  177.0 24.8 %all-to-all-done.5 = bf16[4,48,384]{2,1,0:T(8,128)(2,1)S(1)} async-done(((bf16[4,48,384]{2,1,0:T(8,128)(2,1)}), bf16[4,48,384]{2,1,0:T(8,128)(2,1)S(1)}, u32[]{:S(2)}, u32[]{:S(2)}) %all-to-all-start.5) | async-done | bytes 147488 | tf_op jit(solution)/shard_map/all_to_all | solution.py:19
  201.8 4.9 %all-to-all-start.4 = ((bf16[8,72,128]{2,1,0:T(8,128)(2,1)}), bf16[8,72,128]{2,1,0:T(8,128)(2,1)S(1)}, u32[]{:S(2)}, u32[]{:S(2)}) async-start(bf16[8,72,128]{2,1,0:T(8,128)(2,1)} %pad_maximum_fusion.3), calls=%async_computation.4 | async-start | bytes 294912 | tf_op jit(solution)/shard_map/all_to_all | solution.py:19
  207.3 27.9 %all-to-all-done.4 = bf16[8,72,128]{2,1,0:T(8,128)(2,1)S(1)} async-done(((bf16[8,72,128]{2,1,0:T(8,128)(2,1)}), bf16[8,72,128]{2,1,0:T(8,128)(2,1)S(1)}, u32[]{:S(2)}, u32[]{:S(2)}) %all-to-all-start.4) | async-done | bytes 147488 | tf_op jit(solution)/shard_map/all_to_all | solution.py:19
  238.0 15.5 %all_gather.3 = bf16[512,512]{1,0:T(8,128)(2,1)S(1)} all-gather(bf16[128,512]{1,0:T(8,128)(2,1)S(1)} %bitcast.172), channel_id=1, replica_groups=mesh['grp'=2,'wide'=4,'mid'=2,'near'=4,'blk'=4,'pen'=2] {'near'}, dimensions={0}, use_global_device_ids=true | all-gather | bytes 655360 | tf_op jit(solution)/shard_map/all_gather | solution.py:203
  (133 shorter events, 21.4 us)
Async XLA Ops:
  0.6 1.7 copy-start.14
  2.4 1.6 copy-start.10
  5.1 9.4 %copy-start = (bf16[1,512,384]{2,1,0:T(8,128)(2,1)S(1)}, bf16[1,512,384]{2,1,0:T(8,128)(2,1)}, u32[]{:S(2)}) copy-start(bf16[1,512,384]{2,1,0:T(8,128)(2,1)} %param.14) | copy-start | bytes 1179652
  5.1 21.1 %copy-start.15 = (u32[4]{0:T(128)S(1)}, u32[4]{0:T(128)}, u32[]{:S(2)}) copy-start(u32[4]{0:T(128)} %constant.40.clone) | copy-start | bytes 52
  6.0 41.4 %all-to-all-start = ((bf16[4,136,512]{2,1,0:T(8,128)(2,1)}), bf16[4,136,512]{2,1,0:T(8,128)(2,1)S(1)}, u32[]{:S(2)}, u32[]{:S(2)}) async-start(bf16[4,136,512]{2,1,0:T(8,128)(2,1)} %pad_maximum_fusion), calls=%async_computation | async-start | bytes 1114112 | tf_op jit(solution)/shard_map/all_to_all | solution.py:19
  14.5 14.2 %collective-permute-start.2 = (bf16[512,384]{1,0:T(8,128)(2,1)S(1)}, bf16[512,384]{1,0:T(8,128)(2,1)S(1)}, u32[]{:S(2)}, u32[]{:S(2)}) collective-permute-start(bf16[512,384]{1,0:T(8,128)(2,1)S(1)} %bitcast.156), channel_id=1, source_target_pairs={{0,2},{2,4},{4,6},{6,0},{1,3},{3,5},{5,7},{7,1},{8,10},{10,12},{12... | collective-permute-start | bytes 1179656 | tf_op jit(solution)/shard_map/ppermute | solution.py:103
  18.0 20.0 %collective-permute-start.1 = (bf16[512,384]{1,0:T(8,128)(2,1)S(1)}, bf16[512,384]{1,0:T(8,128)(2,1)S(1)}, u32[]{:S(2)}, u32[]{:S(2)}) collective-permute-start(bf16[512,384]{1,0:T(8,128)(2,1)S(1)} %bitcast.157), channel_id=1, source_target_pairs={{0,4},{2,6},{4,0},{6,2},{1,5},{3,7},{5,1},{7,3},{8,12},{10,14},{12... | collective-permute-start | bytes 1179656 | tf_op jit(solution)/shard_map/ppermute | solution.py:103
  23.0 16.5 %collective-permute-start = (bf16[512,384]{1,0:T(8,128)(2,1)S(1)}, bf16[512,384]{1,0:T(8,128)(2,1)S(1)}, u32[]{:S(2)}, u32[]{:S(2)}) collective-permute-start(bf16[512,384]{1,0:T(8,128)(2,1)S(1)} %bitcast.158), channel_id=1, source_target_pairs={{0,6},{2,0},{4,2},{6,4},{1,7},{3,1},{5,3},{7,5},{8,14},{10,8},{12,... | collective-permute-start | bytes 1179656 | tf_op jit(solution)/shard_map/ppermute | solution.py:103
  28.6 10.8 %copy-start.2 = (bf16[512,384]{1,0:T(8,128)(2,1)}, bf16[512,384]{1,0:T(8,128)(2,1)S(1)}, u32[]{:S(2)}) copy-start(bf16[512,384]{1,0:T(8,128)(2,1)S(1)} %collective-permute-done.2.refs_1_) | copy-start | bytes 1179652
  43.6 46.2 %copy-start.8 = (bf16[2,8,48,384]{3,2,1,0:T(8,128)(2,1)S(1)}, bf16[2,8,48,384]{3,2,1,0:T(8,128)(2,1)}, u32[]{:S(2)}) copy-start(bf16[2,8,48,384]{3,2,1,0:T(8,128)(2,1)} %get-tuple-element.8) | copy-start | bytes 1769476
  43.6 45.4 %collective-permute-start.3 = (bf16[2,8,48,384]{3,2,1,0:T(8,128)(2,1)}, bf16[2,8,48,384]{3,2,1,0:T(8,128)(2,1)S(1)}, u32[]{:S(2)}, u32[]{:S(2)}) collective-permute-start(bf16[2,8,48,384]{3,2,1,0:T(8,128)(2,1)} %get-tuple-element.9), channel_id=1, source_target_pairs={{0,8},{8,0},{16,24},{24,16},{1,9},{9,1},{17,25},{25,17},{2,10},{10... | collective-permute-start | bytes 1769480 | tf_op jit(solution)/shard_map/ppermute | solution.py:129
  48.2 76.2 %all-to-all-start.1 = ((bf16[8,24,512]{2,1,0:T(8,128)(2,1)}), bf16[8,24,512]{2,1,0:T(8,128)(2,1)S(1)}, u32[]{:S(2)}, u32[]{:S(2)}) async-start(bf16[8,24,512]{2,1,0:T(8,128)(2,1)} %pad_maximum_fusion.2), calls=%async_computation.1 | async-start | bytes 393216 | tf_op jit(solution)/shard_map/all_to_all | solution.py:19
  89.8 6.4 %copy-start.1 = (bf16[1,512,384]{2,1,0:T(8,128)(2,1)S(1)}, bf16[1,512,384]{2,1,0:T(8,128)(2,1)}, u32[]{:S(2)}) copy-start(bf16[1,512,384]{2,1,0:T(8,128)(2,1)} %param.14) | copy-start | bytes 1179652
  91.2 33.4 %copy-start.11 = (f32[2,512]{1,0:T(2,128)S(1)}, f32[2,512]{1,0:T(2,128)}, u32[]{:S(2)}) copy-start(f32[2,512]{1,0:T(2,128)} %param.10) | copy-start | bytes 12292
  91.2 33.4 %copy-start.13 = (f32[4]{0:T(128)S(1)}, f32[4]{0:T(128)}, u32[]{:S(2)}) copy-start(f32[4]{0:T(128)} %param.11) | copy-start | bytes 52
  91.2 29.2 %collective-permute-start.4 = (bf16[8,48,384]{2,1,0:T(8,128)(2,1)S(1)}, bf16[8,48,384]{2,1,0:T(8,128)(2,1)S(1)}, u32[]{:S(2)}, u32[]{:S(2)}) collective-permute-start(bf16[8,48,384]{2,1,0:T(8,128)(2,1)S(1)} %dynamic-slice_bitcast_fusion), channel_id=1, source_target_pairs={{0,16},{8,24},{16,0},{24,8},{1,17},{9,25},{17,1},{25,9},{2,18},{10... | collective-permute-start | bytes 884744 | tf_op jit(solution)/shard_map/ppermute | solution.py:132
  120.4 10.6 %copy-start.7 = (bf16[512,384]{1,0:T(8,128)(2,1)S(1)}, bf16[512,384]{1,0:T(8,128)(2,1)}, u32[]{:S(2)}) copy-start(bf16[512,384]{1,0:T(8,128)(2,1)} %copy-done.6) | copy-start | bytes 1179652
  124.7 6.6 %copy-start.3 = (bf16[512,384]{1,0:T(8,128)(2,1)S(1)}, bf16[512,384]{1,0:T(8,128)(2,1)}, u32[]{:S(2)}) copy-start(bf16[512,384]{1,0:T(8,128)(2,1)} %copy-done.2) | copy-start | bytes 1179652
  125.0 6.7 %copy-start.5 = (bf16[512,384]{1,0:T(8,128)(2,1)S(1)}, bf16[512,384]{1,0:T(8,128)(2,1)}, u32[]{:S(2)}) copy-start(bf16[512,384]{1,0:T(8,128)(2,1)} %copy-done.4) | copy-start | bytes 1179652
  125.9 10.3 %all-to-all-start.2 = ((bf16[4,8,512]{2,1,0:T(8,128)(2,1)}), bf16[4,8,512]{2,1,0:T(8,128)(2,1)S(1)}, u32[]{:S(2)}, u32[]{:S(2)}) async-start(bf16[4,8,512]{2,1,0:T(8,128)(2,1)} %broadcast_in_dim.28), calls=%async_computation.2 | async-start | bytes 65536 | tf_op jit(solution)/shard_map/all_to_all | solution.py:19
  137.1 22.9 %all-to-all-start.3 = ((f32[4,32,128]{2,1,0:T(8,128)}), f32[4,32,128]{2,1,0:T(8,128)S(1)}, u32[]{:S(2)}, u32[]{:S(2)}) async-start(f32[4,32,128]{2,1,0:T(8,128)} %bitcast.147), calls=%async_computation.3 | async-start | bytes 131072 | tf_op jit(solution)/shard_map/all_to_all | solution.py:19
  143.5 15.7 %collective-permute-start.5 = (bf16[4,48,384]{2,1,0:T(8,128)(2,1)S(1)}, bf16[4,48,384]{2,1,0:T(8,128)(2,1)S(1)}, u32[]{:S(2)}, u32[]{:S(2)}) collective-permute-start(bf16[4,48,384]{2,1,0:T(8,128)(2,1)S(1)} %dynamic-slice_bitcast_fusion.1), channel_id=1, source_target_pairs={{0,32},{32,0},{1,33},{33,1},{2,34},{34,2},{3,35},{35,3},{4,36},{36... | collective-permute-start | bytes 442376 | tf_op jit(solution)/shard_map/ppermute | solution.py:139
  160.0 41.8 %all-to-all-start.5 = ((bf16[4,48,384]{2,1,0:T(8,128)(2,1)}), bf16[4,48,384]{2,1,0:T(8,128)(2,1)S(1)}, u32[]{:S(2)}, u32[]{:S(2)}) async-start(bf16[4,48,384]{2,1,0:T(8,128)(2,1)} %fusion.23), calls=%async_computation.5 | async-start | bytes 294912 | tf_op jit(solution)/shard_map/all_to_all | solution.py:19
  201.8 33.5 %all-to-all-start.4 = ((bf16[8,72,128]{2,1,0:T(8,128)(2,1)}), bf16[8,72,128]{2,1,0:T(8,128)(2,1)S(1)}, u32[]{:S(2)}, u32[]{:S(2)}) async-start(bf16[8,72,128]{2,1,0:T(8,128)(2,1)} %pad_maximum_fusion.3), calls=%async_computation.4 | async-start | bytes 294912 | tf_op jit(solution)/shard_map/all_to_all | solution.py:19
  (4 other events, 4.5 us)

commit v5 on v4

--- a/solution.py
+++ b/solution.py
@@ -133,13 +133,6 @@
     kept = lax.dynamic_index_in_dim(halves, high, 0, keepdims=False)
     gram_local = (kept.astype(F32) + met.astype(F32)).astype(BF)
 
-    part = lax.axis_index("mid").astype(jnp.uint32)
-    gram_local = gram_local.reshape(wide, far // wide, share, old_width)
-    gone = lax.dynamic_index_in_dim(gram_local, part ^ jnp.uint32(1), 1, keepdims=False)
-    met = lax.ppermute(gone, "mid", [(0, 1), (1, 0)])
-    kept = lax.dynamic_index_in_dim(gram_local, part, 1, keepdims=False)
-    gram_local = (kept.astype(F32) + met.astype(F32)).astype(BF)
-
     bulk = block_count * FOLDS * prot_width // near
     slim = block_count * FOLDS
     packed = jnp.concatenate(
@@ -171,19 +164,33 @@
     added = jnp.concatenate([jnp.sum(mask[:, None, :] * f, axis=0) for f in fits_q], axis=0)
     added = added.astype(BF)
     new_width = added.shape[0]
-    new_all = exchange(copies(added, blocks), "blk").reshape(blocks * new_width, row_count)
     target = traits[:1]
-    small = dot(added, jnp.concatenate([new_all, target], axis=0), ((1,), (1,)))
     left = jnp.concatenate([added, target], axis=0)
     turned = [olds[shifts.index(-m % blocks)] for m in range(blocks)]
     cross = jnp.stack([dot(left, old, ((1,), (0,))) for old in turned])
     cross = cross.reshape(blocks, new_width + 1, far // blocks, near, share)
-    cross = jnp.transpose(cross, (3, 0, 2, 1, 4)).reshape(near, far * (new_width + 1) * share)
-    sums = jnp.concatenate([cross, copies(small.reshape(-1), near)], axis=1)
-    width = sums.shape[1]
-    sums = jnp.pad(sums, ((0, 0), (0, -width % (8 * LANES)))).reshape(near, -1, LANES)
-    sums = total(exchange(sums, "near")).reshape(-1)
     cut = (new_width + 1) * share
+    cross = jnp.transpose(cross, (3, 0, 2, 1, 4)).reshape(near, far * cut)
+    fit = dot(added, target, ((1,), (1,))).reshape(1, new_width)
+    sums = jnp.concatenate([cross, jnp.broadcast_to(fit, (near, new_width))], axis=1)
+    sums = jnp.pad(sums, ((0, 0), (0, -sums.shape[1] % (8 * row_count))))
+    sums = sums.astype(BF).reshape(near, -1, row_count)
+    mixed = jnp.concatenate([copies(added, near), sums], axis=1)
+    mixed = jnp.broadcast_to(mixed[:, None], (near, blocks, *mixed.shape[1:]))
+    mixed = exchange(mixed.reshape(near * blocks, *mixed.shape[2:]), ("near", "blk"))
+    mixed = mixed.reshape(near, blocks, *mixed.shape[1:])
+    mine = lax.dynamic_index_in_dim(mixed, place, 1, keepdims=False)
+    sums = total(mine[:, new_width:]).reshape(-1)
+    small = sum(
+        dot(
+            mine[n, :new_width],
+            mixed[n, :, :new_width].reshape(blocks * new_width, row_count),
+            ((1,), (1,)),
+        )
+        for n in range(near)
+    )
+    fit = sums[far * cut : far * cut + new_width].reshape(new_width, 1)
+    small = jnp.concatenate([small, fit], axis=1).reshape(-1).astype(BF)
     cross = sums[: far * cut].astype(BF).reshape(blocks, far // blocks, cut)
     cross = lax.dynamic_slice_in_dim(
         jnp.concatenate([cross, cross]),
@@ -192,7 +199,7 @@
         0,
     )
     sums = jnp.concatenate(
-        [cross.reshape(far, cut), copies(sums[far * cut : width].astype(BF), far)], axis=1
+        [cross.reshape(far, cut), copies(small, far)], axis=1
     )
     width = sums.shape[1]
     sums = jnp.pad(sums, ((0, 0), (0, -width % (8 * LANES)))).reshape(far, -1, LANES)
@@ -202,7 +209,7 @@
     bulk_far = widen(packed[:, : slab.shape[0]], bulk_sum.shape[0]).reshape(bulk, var_width)
     bulk_all = lax.all_gather(bulk_far, "near", axis=0, tiled=True)
     final = (total(packed[:, slab.shape[0] :]) * inverse).reshape(-1)
-    gram_all = exchange(gram_local, "wide")
+    gram_all = exchange(gram_local, away)
     gram_old = total(gram_all).T * inverse
     cross_sum = final[:cut].reshape(new_width + 1, share)
     small_sum = final[cut:width].reshape(new_width, blocks * new_width + 1)

time: 259 us -> 260 us (level)
  blocking collectives: 15.5 us -> 38.8 us
  starting transfers between devices: 106 us -> 87.5 us
  local copies, waits for them, and re-layouts: 7.46 us -> 4.81 us
    all_to_all x6 -> x4, waiting for transfers between devices: 60.8 us -> 86.4 us  [exchange(): return lax.all_to_all(blocks, axis, split_axis=0, concat_axis=0, tiled=True)]
    all_to_all x0 -> x1, blocking collectives: none -> 23.5 us  [exchange(): return lax.all_to_all(blocks, axis, split_axis=0, concat_axis=0, tiled=True)]
    ppermute x1, waiting for transfers between devices: 24 us -> 10.6 us  [per_device(): met = lax.ppermute(gone, 'near', [(i, i ^ 2) for i in range(near)])]
    all_to_all x6 -> x4, starting transfers between devices: 81.4 us -> 68.3 us  [exchange(): return lax.all_to_all(blocks, axis, split_axis=0, concat_axis=0, tiled=True)]
    ppermute x3, waiting for transfers between devices: 12.7 us -> 0.01 us  [per_device(): lax.ppermute(old_cols, 'blk', [(i, (i + s) % blocks) for i in range(block...]
    ppermute x1, waiting for transfers between devices: 0.01 us -> 11.2 us  [per_device(): met = lax.ppermute(gone, 'near', [(i, i ^ 1) for i in range(near)])]
    ppermute x1 -> x0, waiting for transfers between devices: 10.5 us -> none  [per_device(): met = lax.ppermute(gone, 'mid', [(0, 1), (1, 0)])]
    ppermute x1 -> x0, starting transfers between devices: 5.18 us -> none  [per_device(): met = lax.ppermute(gone, 'mid', [(0, 1), (1, 0)])]
  transfers between devices with their start and end apart: 12 -> 9, of which waited for: 9 -> 5; matrix products, arithmetic and copies ran while one was open for 3% -> 3% of each run, Pallas kernels for 1% -> 1%
where the time goes in v5:
time: 260 us
  waiting for transfers between devices  108 us (42%)
  starting transfers between devices  87.5 us (34%)
  blocking collectives  38.8 us (15%)
  matrix products  8.85 us (3%)
  other arithmetic  6.64 us (3%)
  local copies, waits for them, and re-layouts  4.81 us (2%)
  Pallas kernels  3.39 us (1%)
    all_to_all x4, waiting for transfers between devices, exchange(): return lax.all_to_all(blocks, axis, split_axis=0, concat_axis=0, tiled=True)  86.4 us
    all_to_all x4, starting transfers between devices, exchange(): return lax.all_to_all(blocks, axis, split_axis=0, concat_axis=0, tiled=True)  68.3 us
    all_to_all x1, blocking collectives, exchange(): return lax.all_to_all(blocks, axis, split_axis=0, concat_axis=0, tiled=True)  23.5 us
    all_gather x1, blocking collectives, per_device(): bulk_all = lax.all_gather(bulk_far, 'near', axis=0, tiled=True)  15.2 us
    ppermute x3, starting transfers between devices, per_device(): lax.ppermute(old_cols, 'blk', [(i, (i + s) % blocks) for i in range(block...  11.7 us
    ppermute x1, waiting for transfers between devices, per_device(): met = lax.ppermute(gone, 'near', [(i, i ^ 1) for i in range(near)])  11.2 us
    ppermute x1, waiting for transfers between devices, per_device(): met = lax.ppermute(gone, 'near', [(i, i ^ 2) for i in range(near)])  10.6 us
    dot_general x23, matrix products, dot(): lax.dot_general(left, right, (dims, ((), ())), preferred_element_type=F32)  5.62 us
  transfers between devices with their start and end apart: 9, of which 5 were waited for; matrix products, arithmetic and copies ran while one was open for 3% of the time, Pallas kernels for 1%

profile of v5, /device:TPU:40, one launch (start us, length us, event | category | flops | bytes accessed | tf_op | source)
XLA Modules:
  0.0 259.6 jit_solution(7791977247092653164)
XLA Ops:
  0.6 1.7 convolution_convert_fusion
  2.4 1.5 convolution_convert_fusion.1
  5.1 23.5 %all_to_all.25 = bf16[4,136,512]{2,1,0:T(8,128)(2,1)S(1)} all-to-all(bf16[4,136,512]{2,1,0:T(8,128)(2,1)S(1)} %pad_maximum_fusion), channel_id=1, replica_groups=mesh['grp'=2,'wide'=4,'mid'=2,'near'=4,'blk'=4,'pen'=2] {'near'}, dimensions={0} | all-to-all | bytes 1114112 | tf_op jit(solution)/shard_map/all_to_all | solution.py:19
  29.5 40.7 %all-to-all-start.1 = ((bf16[8,24,512]{2,1,0:T(8,128)(2,1)}), bf16[8,24,512]{2,1,0:T(8,128)(2,1)S(1)}, u32[]{:S(2)}, u32[]{:S(2)}) async-start(bf16[8,24,512]{2,1,0:T(8,128)(2,1)} %pad_maximum_fusion.2), calls=%async_computation.1 | async-start | bytes 393216 | tf_op jit(solution)/shard_map/all_to_all | solution.py:19
  70.3 3.6 %collective-permute-start.2 = (bf16[512,384]{1,0:T(8,128)(2,1)S(1)}, bf16[512,384]{1,0:T(8,128)(2,1)S(1)}, u32[]{:S(2)}, u32[]{:S(2)}) collective-permute-start(bf16[512,384]{1,0:T(8,128)(2,1)S(1)} %bitcast.186), channel_id=1, source_target_pairs={{0,2},{2,4},{4,6},{6,0},{1,3},{3,5},{5,7},{7,1},{8,10},{10,12},{12... | collective-permute-start | bytes 1179656 | tf_op jit(solution)/shard_map/ppermute | solution.py:103
  73.9 4.9 %collective-permute-start.1 = (bf16[512,384]{1,0:T(8,128)(2,1)S(1)}, bf16[512,384]{1,0:T(8,128)(2,1)S(1)}, u32[]{:S(2)}, u32[]{:S(2)}) collective-permute-start(bf16[512,384]{1,0:T(8,128)(2,1)S(1)} %bitcast.187), channel_id=1, source_target_pairs={{0,4},{2,6},{4,0},{6,2},{1,5},{3,7},{5,1},{7,3},{8,12},{10,14},{12... | collective-permute-start | bytes 1179656 | tf_op jit(solution)/shard_map/ppermute | solution.py:103
  78.8 3.2 %collective-permute-start = (bf16[512,384]{1,0:T(8,128)(2,1)S(1)}, bf16[512,384]{1,0:T(8,128)(2,1)S(1)}, u32[]{:S(2)}, u32[]{:S(2)}) collective-permute-start(bf16[512,384]{1,0:T(8,128)(2,1)S(1)} %bitcast.188), channel_id=1, source_target_pairs={{0,6},{2,0},{4,2},{6,4},{1,7},{3,1},{5,3},{7,5},{8,14},{10,8},{12,... | collective-permute-start | bytes 1179656 | tf_op jit(solution)/shard_map/ppermute | solution.py:103
  82.3 18.7 %all-to-all-done.1 = bf16[8,24,512]{2,1,0:T(8,128)(2,1)S(1)} async-done(((bf16[8,24,512]{2,1,0:T(8,128)(2,1)}), bf16[8,24,512]{2,1,0:T(8,128)(2,1)S(1)}, u32[]{:S(2)}, u32[]{:S(2)}) %all-to-all-start.1) | async-done | bytes 196640 | tf_op jit(solution)/shard_map/all_to_all | solution.py:19
  103.5 0.8 broadcast_in_dim.30
  104.3 8.4 %all-to-all-start.2 = ((bf16[16,16,512]{2,1,0:T(8,128)(2,1)}), bf16[16,16,512]{2,1,0:T(8,128)(2,1)S(1)}, u32[]{:S(2)}, u32[]{:S(2)}) async-start(bf16[16,16,512]{2,1,0:T(8,128)(2,1)} %bitcast.23), calls=%async_computation.2 | async-start | bytes 524288 | tf_op jit(solution)/shard_map/all_to_all | solution.py:19
  113.2 3.4 %paired_gram.1 = (bf16[2,8,48,384]{3,2,1,0:T(8,128)(2,1)}, bf16[2,8,48,384]{3,2,1,0:T(8,128)(2,1)}) custom-call(s32[1]{0:T(128)} %bitcast.61.side_ref, s32[4]{0:T(128)} %and_convert_fusion.spots_ref, bf16[512,384]{1,0:T(8,128)(2,1)} %bitcast.185, bf16[512,384]{1,0:T(8,128)(2,1)} %copy-done.1, bf16[512,384]{1,0:T(8,128)(2,1)} %copy-done.3, ...), custom_call_target="tpu_custom_call" | custom-call | tf_op jit(solution)/shard_map/paired_gram/pallas_call | solution.py:58
  116.6 3.6 %collective-permute-start.3 = (bf16[2,8,48,384]{3,2,1,0:T(8,128)(2,1)}, bf16[2,8,48,384]{3,2,1,0:T(8,128)(2,1)S(1)}, u32[]{:S(2)}, u32[]{:S(2)}) collective-permute-start(bf16[2,8,48,384]{3,2,1,0:T(8,128)(2,1)} %get-tuple-element.9), channel_id=1, source_target_pairs={{0,8},{8,0},{16,24},{24,16},{1,9},{9,1},{17,25},{25,17},{2,10},{10... | collective-permute-start | bytes 1769480 | tf_op jit(solution)/shard_map/ppermute | solution.py:129
  120.3 11.2 %collective-permute-done.3 = bf16[2,8,48,384]{3,2,1,0:T(8,128)(2,1)S(1)} collective-permute-done((bf16[2,8,48,384]{3,2,1,0:T(8,128)(2,1)}, bf16[2,8,48,384]{3,2,1,0:T(8,128)(2,1)S(1)}, u32[]{:S(2)}, u32[]{:S(2)}) %collective-permute-start.3) | collective-permute-done | bytes 589856 | tf_op jit(solution)/shard_map/ppermute | solution.py:129
  131.5 1.2 add_convert_fusion
  132.8 3.9 %collective-permute-start.4 = (bf16[8,48,384]{2,1,0:T(8,128)(2,1)S(1)}, bf16[8,48,384]{2,1,0:T(8,128)(2,1)S(1)}, u32[]{:S(2)}, u32[]{:S(2)}) collective-permute-start(bf16[8,48,384]{2,1,0:T(8,128)(2,1)S(1)} %dynamic-slice_bitcast_fusion), channel_id=1, source_target_pairs={{0,16},{8,24},{16,0},{24,8},{1,17},{9,25},{17,1},{25,9},{2,18},{10... | collective-permute-start | bytes 884744 | tf_op jit(solution)/shard_map/ppermute | solution.py:132
  136.7 10.6 %collective-permute-done.4 = bf16[8,48,384]{2,1,0:T(8,128)(2,1)S(1)} collective-permute-done((bf16[8,48,384]{2,1,0:T(8,128)(2,1)S(1)}, bf16[8,48,384]{2,1,0:T(8,128)(2,1)S(1)}, u32[]{:S(2)}, u32[]{:S(2)}) %collective-permute-start.4) | collective-permute-done | bytes 294944 | tf_op jit(solution)/shard_map/ppermute | solution.py:132
  147.3 0.8 fusion.17
  148.1 14.4 %all-to-all-start.4 = ((bf16[8,48,384]{2,1,0:T(8,128)(2,1)}), bf16[8,48,384]{2,1,0:T(8,128)(2,1)S(1)}, u32[]{:S(2)}, u32[]{:S(2)}) async-start(bf16[8,48,384]{2,1,0:T(8,128)(2,1)} %fusion.17), calls=%async_computation.4 | async-start | bytes 589824 | tf_op jit(solution)/shard_map/all_to_all | solution.py:19
  164.4 37.9 %all-to-all-done.4 = bf16[8,48,384]{2,1,0:T(8,128)(2,1)S(1)} async-done(((bf16[8,48,384]{2,1,0:T(8,128)(2,1)}), bf16[8,48,384]{2,1,0:T(8,128)(2,1)S(1)}, u32[]{:S(2)}, u32[]{:S(2)}) %all-to-all-start.4) | async-done | bytes 294944 | tf_op jit(solution)/shard_map/all_to_all | solution.py:19
  202.3 4.7 %all-to-all-start.3 = ((bf16[8,72,128]{2,1,0:T(8,128)(2,1)}), bf16[8,72,128]{2,1,0:T(8,128)(2,1)S(1)}, u32[]{:S(2)}, u32[]{:S(2)}) async-start(bf16[8,72,128]{2,1,0:T(8,128)(2,1)} %pad_maximum_fusion.3), calls=%async_computation.3 | async-start | bytes 294912 | tf_op jit(solution)/shard_map/all_to_all | solution.py:19
  207.7 29.7 %all-to-all-done.3 = bf16[8,72,128]{2,1,0:T(8,128)(2,1)S(1)} async-done(((bf16[8,72,128]{2,1,0:T(8,128)(2,1)}), bf16[8,72,128]{2,1,0:T(8,128)(2,1)S(1)}, u32[]{:S(2)}, u32[]{:S(2)}) %all-to-all-start.3) | async-done | bytes 147488 | tf_op jit(solution)/shard_map/all_to_all | solution.py:19
  238.1 0.7 slice_reduce_fusion.1
  240.1 15.2 %all_gather.3 = bf16[512,512]{1,0:T(8,128)(2,1)S(1)} all-gather(bf16[128,512]{1,0:T(8,128)(2,1)S(1)} %bitcast.205), channel_id=1, replica_groups=mesh['grp'=2,'wide'=4,'mid'=2,'near'=4,'blk'=4,'pen'=2] {'near'}, dimensions={0}, use_global_device_ids=true | all-gather | bytes 655360 | tf_op jit(solution)/shard_map/all_gather | solution.py:210
  258.7 0.8 maximum_bitcast_fusion
  (124 shorter events, 12.8 us)
Async XLA Ops:
  0.6 1.7 copy-start.8
  2.4 1.5 copy-start.6
  2.4 1.6 copy-start.4
  28.7 41.6 %copy-start = (bf16[1,512,384]{2,1,0:T(8,128)(2,1)S(1)}, bf16[1,512,384]{2,1,0:T(8,128)(2,1)}, u32[]{:S(2)}) copy-start(bf16[1,512,384]{2,1,0:T(8,128)(2,1)} %param.14) | copy-start | bytes 1179652
  28.8 72.3 %copy-start.5 = (f32[2,512]{1,0:T(2,128)S(1)}, f32[2,512]{1,0:T(2,128)}, u32[]{:S(2)}) copy-start(f32[2,512]{1,0:T(2,128)} %param.10) | copy-start | bytes 12292
  28.8 72.3 %copy-start.7 = (f32[4]{0:T(128)S(1)}, f32[4]{0:T(128)}, u32[]{:S(2)}) copy-start(f32[4]{0:T(128)} %param.11) | copy-start | bytes 52
  29.5 71.5 %all-to-all-start.1 = ((bf16[8,24,512]{2,1,0:T(8,128)(2,1)}), bf16[8,24,512]{2,1,0:T(8,128)(2,1)S(1)}, u32[]{:S(2)}, u32[]{:S(2)}) async-start(bf16[8,24,512]{2,1,0:T(8,128)(2,1)} %pad_maximum_fusion.2), calls=%async_computation.1 | async-start | bytes 393216 | tf_op jit(solution)/shard_map/all_to_all | solution.py:19
  70.3 32.5 %collective-permute-start.2 = (bf16[512,384]{1,0:T(8,128)(2,1)S(1)}, bf16[512,384]{1,0:T(8,128)(2,1)S(1)}, u32[]{:S(2)}, u32[]{:S(2)}) collective-permute-start(bf16[512,384]{1,0:T(8,128)(2,1)S(1)} %bitcast.186), channel_id=1, source_target_pairs={{0,2},{2,4},{4,6},{6,0},{1,3},{3,5},{5,7},{7,1},{8,10},{10,12},{12... | collective-permute-start | bytes 1179656 | tf_op jit(solution)/shard_map/ppermute | solution.py:103
  73.9 27.9 %collective-permute-start.1 = (bf16[512,384]{1,0:T(8,128)(2,1)S(1)}, bf16[512,384]{1,0:T(8,128)(2,1)S(1)}, u32[]{:S(2)}, u32[]{:S(2)}) collective-permute-start(bf16[512,384]{1,0:T(8,128)(2,1)S(1)} %bitcast.187), channel_id=1, source_target_pairs={{0,4},{2,6},{4,0},{6,2},{1,5},{3,7},{5,1},{7,3},{8,12},{10,14},{12... | collective-permute-start | bytes 1179656 | tf_op jit(solution)/shard_map/ppermute | solution.py:103
  78.8 23.1 %collective-permute-start = (bf16[512,384]{1,0:T(8,128)(2,1)S(1)}, bf16[512,384]{1,0:T(8,128)(2,1)S(1)}, u32[]{:S(2)}, u32[]{:S(2)}) collective-permute-start(bf16[512,384]{1,0:T(8,128)(2,1)S(1)} %bitcast.188), channel_id=1, source_target_pairs={{0,6},{2,0},{4,2},{6,4},{1,7},{3,1},{5,3},{7,5},{8,14},{10,8},{12,... | collective-permute-start | bytes 1179656 | tf_op jit(solution)/shard_map/ppermute | solution.py:103
  101.8 1.4 copy-start.2
  101.9 1.4 copy-start.3
  102.8 1.5 copy-start.1
  103.1 9.6 %copy-start.9 = (u32[4]{0:T(128)S(1)}, u32[4]{0:T(128)}, u32[]{:S(2)}) copy-start(u32[4]{0:T(128)} %constant.36.clone) | copy-start | bytes 52
  104.3 43.9 %all-to-all-start.2 = ((bf16[16,16,512]{2,1,0:T(8,128)(2,1)}), bf16[16,16,512]{2,1,0:T(8,128)(2,1)S(1)}, u32[]{:S(2)}, u32[]{:S(2)}) async-start(bf16[16,16,512]{2,1,0:T(8,128)(2,1)} %bitcast.23), calls=%async_computation.2 | async-start | bytes 524288 | tf_op jit(solution)/shard_map/all_to_all | solution.py:19
  116.6 14.9 %collective-permute-start.3 = (bf16[2,8,48,384]{3,2,1,0:T(8,128)(2,1)}, bf16[2,8,48,384]{3,2,1,0:T(8,128)(2,1)S(1)}, u32[]{:S(2)}, u32[]{:S(2)}) collective-permute-start(bf16[2,8,48,384]{3,2,1,0:T(8,128)(2,1)} %get-tuple-element.9), channel_id=1, source_target_pairs={{0,8},{8,0},{16,24},{24,16},{1,9},{9,1},{17,25},{25,17},{2,10},{10... | collective-permute-start | bytes 1769480 | tf_op jit(solution)/shard_map/ppermute | solution.py:129
  132.8 14.5 %collective-permute-start.4 = (bf16[8,48,384]{2,1,0:T(8,128)(2,1)S(1)}, bf16[8,48,384]{2,1,0:T(8,128)(2,1)S(1)}, u32[]{:S(2)}, u32[]{:S(2)}) collective-permute-start(bf16[8,48,384]{2,1,0:T(8,128)(2,1)S(1)} %dynamic-slice_bitcast_fusion), channel_id=1, source_target_pairs={{0,16},{8,24},{16,0},{24,8},{1,17},{9,25},{17,1},{25,9},{2,18},{10... | collective-permute-start | bytes 884744 | tf_op jit(solution)/shard_map/ppermute | solution.py:132
  148.1 54.2 %all-to-all-start.4 = ((bf16[8,48,384]{2,1,0:T(8,128)(2,1)}), bf16[8,48,384]{2,1,0:T(8,128)(2,1)S(1)}, u32[]{:S(2)}, u32[]{:S(2)}) async-start(bf16[8,48,384]{2,1,0:T(8,128)(2,1)} %fusion.17), calls=%async_computation.4 | async-start | bytes 589824 | tf_op jit(solution)/shard_map/all_to_all | solution.py:19
  202.3 35.1 %all-to-all-start.3 = ((bf16[8,72,128]{2,1,0:T(8,128)(2,1)}), bf16[8,72,128]{2,1,0:T(8,128)(2,1)S(1)}, u32[]{:S(2)}, u32[]{:S(2)}) async-start(bf16[8,72,128]{2,1,0:T(8,128)(2,1)} %pad_maximum_fusion.3), calls=%async_computation.3 | async-start | bytes 294912 | tf_op jit(solution)/shard_map/all_to_all | solution.py:19

commit v6 on v5

--- a/solution.py
+++ b/solution.py
@@ -203,14 +203,14 @@
     )
     width = sums.shape[1]
     sums = jnp.pad(sums, ((0, 0), (0, -width % (8 * LANES)))).reshape(far, -1, LANES)
-    slab = narrow(bulk_sum)
-    packed = jnp.concatenate([copies(slab, far), sums], axis=1)
+    mid = sums.shape[1]
+    packed = jnp.concatenate([sums, narrow(gram_local)], axis=1)
     packed = exchange(packed, away)
-    bulk_far = widen(packed[:, : slab.shape[0]], bulk_sum.shape[0]).reshape(bulk, var_width)
-    bulk_all = lax.all_gather(bulk_far, "near", axis=0, tiled=True)
-    final = (total(packed[:, slab.shape[0] :]) * inverse).reshape(-1)
-    gram_all = exchange(gram_local, away)
-    gram_old = total(gram_all).T * inverse
+    bulk_all = lax.all_gather(bulk_sum, (*away, "near"), axis=0)
+    bulk_all = bulk_all.reshape(far, near, *bulk_sum.shape)
+    bulk_all = jnp.moveaxis(bulk_all, 1, 0)
+    final = (total(packed[:, :mid]) * inverse).reshape(-1)
+    gram_old = widen(total(packed[:, mid:]), share).T * inverse
     cross_sum = final[:cut].reshape(new_width + 1, share)
     small_sum = final[cut:width].reshape(new_width, blocks * new_width + 1)
     crossed = bulk_all.reshape(block_count, FOLDS, prot_width, var_width).astype(F32)

time: 260 us -> 261 us (level)
  the two profiles are of different devices: /device:TPU:40 before, /device:TPU:104 now
where the time goes in v6:
time: 261 us; the launch traced here: 260 us
  starting transfers between devices  82.4 us (32%)
  blocking collectives  81.3 us (31%)
  waiting for transfers between devices  64.6 us (25%)
  matrix products  11.8 us (5%)
  local copies, waits for them, and re-layouts  8.44 us (3%)
  other arithmetic  6.18 us (2%)
  Pallas kernels  3.42 us (1%)
    all_to_all x3, starting transfers between devices, exchange(): return lax.all_to_all(blocks, axis, split_axis=0, concat_axis=0, tiled=True)  64.1 us
    all_gather x1, blocking collectives, per_device(): bulk_all = lax.all_gather(bulk_sum, (*away, 'near'), axis=0)  60 us
    all_to_all x3, waiting for transfers between devices, exchange(): return lax.all_to_all(blocks, axis, split_axis=0, concat_axis=0, tiled=True)  29.4 us
    all_to_all x1, blocking collectives, exchange(): return lax.all_to_all(blocks, axis, split_axis=0, concat_axis=0, tiled=True)  21.2 us
    ppermute x3, waiting for transfers between devices, per_device(): lax.ppermute(old_cols, 'blk', [(i, (i + s) % blocks) for i in range(block...  15.1 us
    ppermute x1, waiting for transfers between devices, per_device(): met = lax.ppermute(gone, 'near', [(i, i ^ 1) for i in range(near)])  12.8 us
    ppermute x3, starting transfers between devices, per_device(): lax.ppermute(old_cols, 'blk', [(i, (i + s) % blocks) for i in range(block...  10.5 us
    dot_general x23, matrix products, dot(): lax.dot_general(left, right, (dims, ((), ())), preferred_element_type=F32)  8.58 us
  transfers between devices with their start and end apart: 8, of which 6 were waited for; matrix products, arithmetic and copies ran while one was open for 4% of the time, Pallas kernels for 1%

profile of v6, /device:TPU:104, one launch (start us, length us, event | category | flops | bytes accessed | tf_op | source)
XLA Modules:
  0.0 259.6 jit_solution(14270194461319453130)
XLA Ops:
  0.6 1.7 convolution_convert_fusion.1
  2.4 1.5 convolution_convert_fusion
  5.1 21.2 %all_to_all.20 = bf16[4,136,512]{2,1,0:T(8,128)(2,1)S(1)} all-to-all(bf16[4,136,512]{2,1,0:T(8,128)(2,1)S(1)} %pad_maximum_fusion), channel_id=1, replica_groups=mesh['grp'=2,'wide'=4,'mid'=2,'near'=4,'blk'=4,'pen'=2] {'near'}, dimensions={0} | all-to-all | bytes 1114112 | tf_op jit(solution)/shard_map/all_to_all | solution.py:19
  27.2 40.9 %all-to-all-start.1 = ((bf16[8,24,512]{2,1,0:T(8,128)(2,1)}), bf16[8,24,512]{2,1,0:T(8,128)(2,1)S(1)}, u32[]{:S(2)}, u32[]{:S(2)}) async-start(bf16[8,24,512]{2,1,0:T(8,128)(2,1)} %pad_maximum_fusion.3), calls=%async_computation.1 | async-start | bytes 393216 | tf_op jit(solution)/shard_map/all_to_all | solution.py:19
  68.1 5.1 %collective-permute-start = (bf16[512,384]{1,0:T(8,128)(2,1)S(1)}, bf16[512,384]{1,0:T(8,128)(2,1)S(1)}, u32[]{:S(2)}, u32[]{:S(2)}) collective-permute-start(bf16[512,384]{1,0:T(8,128)(2,1)S(1)} %bitcast.189), channel_id=1, source_target_pairs={{0,6},{2,0},{4,2},{6,4},{1,7},{3,1},{5,3},{7,5},{8,14},{10,8},{12,... | collective-permute-start | bytes 1179656 | tf_op jit(solution)/shard_map/ppermute | solution.py:103
  73.2 2.5 collective-permute-start.1
  75.7 3.0 %collective-permute-start.2 = (bf16[512,384]{1,0:T(8,128)(2,1)S(1)}, bf16[512,384]{1,0:T(8,128)(2,1)S(1)}, u32[]{:S(2)}, u32[]{:S(2)}) collective-permute-start(bf16[512,384]{1,0:T(8,128)(2,1)S(1)} %bitcast.191), channel_id=1, source_target_pairs={{0,2},{2,4},{4,6},{6,0},{1,3},{3,5},{5,7},{7,1},{8,10},{10,12},{12... | collective-permute-start | bytes 1179656 | tf_op jit(solution)/shard_map/ppermute | solution.py:103
  79.2 9.4 %collective-permute-done.refs_2_ = bf16[512,384]{1,0:T(8,128)(2,1)S(1)} collective-permute-done((bf16[512,384]{1,0:T(8,128)(2,1)S(1)}, bf16[512,384]{1,0:T(8,128)(2,1)S(1)}, u32[]{:S(2)}, u32[]{:S(2)}) %collective-permute-start) | collective-permute-done | bytes 393248 | tf_op jit(solution)/shard_map/ppermute | solution.py:103
  88.7 5.6 %collective-permute-done.2.refs_1_ = bf16[512,384]{1,0:T(8,128)(2,1)S(1)} collective-permute-done((bf16[512,384]{1,0:T(8,128)(2,1)S(1)}, bf16[512,384]{1,0:T(8,128)(2,1)S(1)}, u32[]{:S(2)}, u32[]{:S(2)}) %collective-permute-start.2) | collective-permute-done | bytes 393248 | tf_op jit(solution)/shard_map/ppermute | solution.py:103
  95.0 3.4 %paired_gram.1 = (bf16[2,8,48,384]{3,2,1,0:T(8,128)(2,1)}, bf16[2,8,48,384]{3,2,1,0:T(8,128)(2,1)}) custom-call(s32[1]{0:T(128)} %bitcast.62.side_ref, s32[4]{0:T(128)} %and_convert_fusion.spots_ref, bf16[512,384]{1,0:T(8,128)(2,1)} %bitcast.188, bf16[512,384]{1,0:T(8,128)(2,1)} %copy-done.2, bf16[512,384]{1,0:T(8,128)(2,1)} %copy-done.6, ...), custom_call_target="tpu_custom_call" | custom-call | tf_op jit(solution)/shard_map/paired_gram/pallas_call | solution.py:58
  98.4 4.0 %collective-permute-start.3 = (bf16[2,8,48,384]{3,2,1,0:T(8,128)(2,1)}, bf16[2,8,48,384]{3,2,1,0:T(8,128)(2,1)S(1)}, u32[]{:S(2)}, u32[]{:S(2)}) collective-permute-start(bf16[2,8,48,384]{3,2,1,0:T(8,128)(2,1)} %get-tuple-element.9), channel_id=1, source_target_pairs={{0,8},{8,0},{16,24},{24,16},{1,9},{9,1},{17,25},{25,17},{2,10},{10... | collective-permute-start | bytes 1769480 | tf_op jit(solution)/shard_map/ppermute | solution.py:129
  103.4 12.8 %collective-permute-done.3 = bf16[2,8,48,384]{3,2,1,0:T(8,128)(2,1)S(1)} collective-permute-done((bf16[2,8,48,384]{3,2,1,0:T(8,128)(2,1)}, bf16[2,8,48,384]{3,2,1,0:T(8,128)(2,1)S(1)}, u32[]{:S(2)}, u32[]{:S(2)}) %collective-permute-start.3) | collective-permute-done | bytes 589856 | tf_op jit(solution)/shard_map/ppermute | solution.py:129
  117.0 3.9 %collective-permute-start.4 = (bf16[8,48,384]{2,1,0:T(8,128)(2,1)}, bf16[8,48,384]{2,1,0:T(8,128)(2,1)}, u32[]{:S(2)}, u32[]{:S(2)}) collective-permute-start(bf16[8,48,384]{2,1,0:T(8,128)(2,1)} %dynamic-slice_bitcast_fusion), channel_id=1, source_target_pairs={{0,16},{8,24},{16,0},{24,8},{1,17},{9,25},{17,1},{25,9},{2,18},{10... | collective-permute-start | bytes 884744 | tf_op jit(solution)/shard_map/ppermute | solution.py:132
  124.0 4.7 %all-to-all-start.2 = ((bf16[16,16,512]{2,1,0:T(8,128)(2,1)}), bf16[16,16,512]{2,1,0:T(8,128)(2,1)}, u32[]{:S(2)}, u32[]{:S(2)}) async-start(bf16[16,16,512]{2,1,0:T(8,128)(2,1)} %bitcast.50), calls=%async_computation.2 | async-start | bytes 524288 | tf_op jit(solution)/shard_map/all_to_all | solution.py:19
  128.7 7.4 %collective-permute-done.4 = bf16[8,48,384]{2,1,0:T(8,128)(2,1)} collective-permute-done((bf16[8,48,384]{2,1,0:T(8,128)(2,1)}, bf16[8,48,384]{2,1,0:T(8,128)(2,1)}, u32[]{:S(2)}, u32[]{:S(2)}) %collective-permute-start.4) | collective-permute-done | bytes 294944 | tf_op jit(solution)/shard_map/ppermute | solution.py:132
  136.1 1.0 fusion.17
  137.2 60.0 %all-gather = bf16[512,512]{1,0:T(8,128)(2,1)S(1)} all-gather(bf16[16,512]{1,0:T(8,128)(2,1)S(1)} %slice.320), channel_id=2, replica_groups=mesh['grp'=2,'wide'=4,'mid'=2,'near'=4,'blk'=4,'pen'=2] {'wide','mid','n..., dimensions={0}, use_global_device_ids=true | all-gather | bytes 540672 | tf_op jit(solution)/shard_map/all_gather | solution.py:209
  199.0 0.9 dynamic-slice_bitcast_fusion.1
  199.9 0.9 fusion.27
  200.8 0.9 convolution_add_fusion.2
  201.6 0.9 convolution_add_fusion.1
  202.5 0.9 fusion.15
  204.7 18.5 %all-to-all-start.3 = ((bf16[8,152,128]{2,1,0:T(8,128)(2,1)}), bf16[8,152,128]{2,1,0:T(8,128)(2,1)S(1)}, u32[]{:S(2)}, u32[]{:S(2)}) async-start(bf16[8,152,128]{2,1,0:T(8,128)(2,1)} %pad_maximum_fusion.2), calls=%async_computation.3 | async-start | bytes 622592 | tf_op jit(solution)/shard_map/all_to_all | solution.py:19
  226.8 29.4 %all-to-all-done.3 = bf16[8,152,128]{2,1,0:T(8,128)(2,1)S(1)} async-done(((bf16[8,152,128]{2,1,0:T(8,128)(2,1)}), bf16[8,152,128]{2,1,0:T(8,128)(2,1)S(1)}, u32[]{:S(2)}, u32[]{:S(2)}) %all-to-all-start.3) | async-done | bytes 311328 | tf_op jit(solution)/shard_map/all_to_all | solution.py:19
  (135 shorter events, 17.9 us)
Async XLA Ops:
  0.6 1.7 copy-start.15
  2.4 1.5 copy-start.13
  2.4 1.6 copy-start.9
  26.4 41.7 %copy-start = (bf16[1,512,384]{2,1,0:T(8,128)(2,1)S(1)}, bf16[1,512,384]{2,1,0:T(8,128)(2,1)}, u32[]{:S(2)}) copy-start(bf16[1,512,384]{2,1,0:T(8,128)(2,1)} %param.14) | copy-start | bytes 1179652
  26.4 52.3 %copy-start.16 = (u32[4]{0:T(128)S(1)}, u32[4]{0:T(128)}, u32[]{:S(2)}) copy-start(u32[4]{0:T(128)} %constant.36.clone) | copy-start | bytes 52
  27.2 75.2 %copy-start.1 = (bf16[1,512,384]{2,1,0:T(8,128)(2,1)S(1)}, bf16[1,512,384]{2,1,0:T(8,128)(2,1)}, u32[]{:S(2)}) copy-start(bf16[1,512,384]{2,1,0:T(8,128)(2,1)} %param.14) | copy-start | bytes 1179652
  27.2 93.7 %all-to-all-start.1 = ((bf16[8,24,512]{2,1,0:T(8,128)(2,1)}), bf16[8,24,512]{2,1,0:T(8,128)(2,1)S(1)}, u32[]{:S(2)}, u32[]{:S(2)}) async-start(bf16[8,24,512]{2,1,0:T(8,128)(2,1)} %pad_maximum_fusion.3), calls=%async_computation.1 | async-start | bytes 393216 | tf_op jit(solution)/shard_map/all_to_all | solution.py:19
  68.1 20.5 %collective-permute-start = (bf16[512,384]{1,0:T(8,128)(2,1)S(1)}, bf16[512,384]{1,0:T(8,128)(2,1)S(1)}, u32[]{:S(2)}, u32[]{:S(2)}) collective-permute-start(bf16[512,384]{1,0:T(8,128)(2,1)S(1)} %bitcast.189), channel_id=1, source_target_pairs={{0,6},{2,0},{4,2},{6,4},{1,7},{3,1},{5,3},{7,5},{8,14},{10,8},{12,... | collective-permute-start | bytes 1179656 | tf_op jit(solution)/shard_map/ppermute | solution.py:103
  73.2 15.5 %collective-permute-start.1 = (bf16[512,384]{1,0:T(8,128)(2,1)S(1)}, bf16[512,384]{1,0:T(8,128)(2,1)S(1)}, u32[]{:S(2)}, u32[]{:S(2)}) collective-permute-start(bf16[512,384]{1,0:T(8,128)(2,1)S(1)} %bitcast.190), channel_id=1, source_target_pairs={{0,4},{2,6},{4,0},{6,2},{1,5},{3,7},{5,1},{7,3},{8,12},{10,14},{12... | collective-permute-start | bytes 1179656 | tf_op jit(solution)/shard_map/ppermute | solution.py:103
  75.7 18.6 %collective-permute-start.2 = (bf16[512,384]{1,0:T(8,128)(2,1)S(1)}, bf16[512,384]{1,0:T(8,128)(2,1)S(1)}, u32[]{:S(2)}, u32[]{:S(2)}) collective-permute-start(bf16[512,384]{1,0:T(8,128)(2,1)S(1)} %bitcast.191), channel_id=1, source_target_pairs={{0,2},{2,4},{4,6},{6,0},{1,3},{3,5},{5,7},{7,1},{8,10},{10,12},{12... | collective-permute-start | bytes 1179656 | tf_op jit(solution)/shard_map/ppermute | solution.py:103
  88.6 5.7 %copy-start.6 = (bf16[512,384]{1,0:T(8,128)(2,1)}, bf16[512,384]{1,0:T(8,128)(2,1)S(1)}, u32[]{:S(2)}) copy-start(bf16[512,384]{1,0:T(8,128)(2,1)S(1)} %collective-permute-done.refs_2_) | copy-start | bytes 1179652
  88.7 5.6 %copy-start.4 = (bf16[512,384]{1,0:T(8,128)(2,1)}, bf16[512,384]{1,0:T(8,128)(2,1)S(1)}, u32[]{:S(2)}) copy-start(bf16[512,384]{1,0:T(8,128)(2,1)S(1)} %collective-permute-done.1.refs_3_) | copy-start | bytes 1179652
  94.3 0.7 copy-start.2
  95.0 7.6 %copy-start.12 = (f32[2,512]{1,0:T(2,128)S(1)}, f32[2,512]{1,0:T(2,128)}, u32[]{:S(2)}) copy-start(f32[2,512]{1,0:T(2,128)} %param.10) | copy-start | bytes 12292
  95.0 7.7 %copy-start.14 = (f32[4]{0:T(128)S(1)}, f32[4]{0:T(128)}, u32[]{:S(2)}) copy-start(f32[4]{0:T(128)} %param.11) | copy-start | bytes 52
  98.4 17.7 %copy-start.8 = (bf16[2,8,48,384]{3,2,1,0:T(8,128)(2,1)S(1)}, bf16[2,8,48,384]{3,2,1,0:T(8,128)(2,1)}, u32[]{:S(2)}) copy-start(bf16[2,8,48,384]{3,2,1,0:T(8,128)(2,1)} %get-tuple-element.8) | copy-start | bytes 1769476
  98.4 17.7 %collective-permute-start.3 = (bf16[2,8,48,384]{3,2,1,0:T(8,128)(2,1)}, bf16[2,8,48,384]{3,2,1,0:T(8,128)(2,1)S(1)}, u32[]{:S(2)}, u32[]{:S(2)}) collective-permute-start(bf16[2,8,48,384]{3,2,1,0:T(8,128)(2,1)} %get-tuple-element.9), channel_id=1, source_target_pairs={{0,8},{8,0},{16,24},{24,16},{1,9},{9,1},{17,25},{25,17},{2,10},{10... | collective-permute-start | bytes 1769480 | tf_op jit(solution)/shard_map/ppermute | solution.py:129
  116.3 5.4 %copy-start.7 = (bf16[512,384]{1,0:T(8,128)(2,1)S(1)}, bf16[512,384]{1,0:T(8,128)(2,1)}, u32[]{:S(2)}) copy-start(bf16[512,384]{1,0:T(8,128)(2,1)} %copy-done.6) | copy-start | bytes 1179652
  117.0 5.0 %copy-start.5 = (bf16[512,384]{1,0:T(8,128)(2,1)S(1)}, bf16[512,384]{1,0:T(8,128)(2,1)}, u32[]{:S(2)}) copy-start(bf16[512,384]{1,0:T(8,128)(2,1)} %copy-done.4) | copy-start | bytes 1179652
  117.0 19.1 %collective-permute-start.4 = (bf16[8,48,384]{2,1,0:T(8,128)(2,1)}, bf16[8,48,384]{2,1,0:T(8,128)(2,1)}, u32[]{:S(2)}, u32[]{:S(2)}) collective-permute-start(bf16[8,48,384]{2,1,0:T(8,128)(2,1)} %dynamic-slice_bitcast_fusion), channel_id=1, source_target_pairs={{0,16},{8,24},{16,0},{24,8},{1,17},{9,25},{17,1},{25,9},{2,18},{10... | collective-permute-start | bytes 884744 | tf_op jit(solution)/shard_map/ppermute | solution.py:132
  121.0 1.3 copy-start.3
  124.0 75.0 %all-to-all-start.2 = ((bf16[16,16,512]{2,1,0:T(8,128)(2,1)}), bf16[16,16,512]{2,1,0:T(8,128)(2,1)}, u32[]{:S(2)}, u32[]{:S(2)}) async-start(bf16[16,16,512]{2,1,0:T(8,128)(2,1)} %bitcast.50), calls=%async_computation.2 | async-start | bytes 524288 | tf_op jit(solution)/shard_map/all_to_all | solution.py:19
  197.7 0.7 copy-start.11
  204.7 51.5 %all-to-all-start.3 = ((bf16[8,152,128]{2,1,0:T(8,128)(2,1)}), bf16[8,152,128]{2,1,0:T(8,128)(2,1)S(1)}, u32[]{:S(2)}, u32[]{:S(2)}) async-start(bf16[8,152,128]{2,1,0:T(8,128)(2,1)} %pad_maximum_fusion.2), calls=%async_computation.3 | async-start | bytes 622592 | tf_op jit(solution)/shard_map/all_to_all | solution.py:19
  (1 other events, 0.7 us)
